TPU v7x, 32 devices: a whole 2x2x4 slice. The times are simulated.
32 devices in a mesh: rows: 8 (over z, y), rep: 4 (over x, core).
Axes of the slice: x: 2, y: 2, z: 4, core: 2. Of those that a mesh axis runs over, the one named last changes fastest.
Arguments:
- event_slots: int32 [32, 128], P(('rows', 'rep')), may hold values from 0 to 143, as said below
- fetch_rows: int32 [32, 16], P(('rows', 'rep')), may hold values from 0 to 255, as said below
- fetch_counts: int32 [32, 8], P(('rows', 'rep')), may hold values from 1 to 2, as said below
- hot_table: float32 [128, 512], replicated, may hold values from -6 to 6
- hot_accum: float32 [128], replicated, may hold values from 0.05 to 2
- cold_table: float32 [2048, 512], P('rows'), may hold values from -6 to 6
- cold_accum: float32 [2048], P('rows'), may hold values from 0.05 to 2
- ln_gain: float32 [512], replicated, may hold values from 0.1 to 1.9
- ln_bias: float32 [512], replicated, may hold values from -3 to 3
- w_in: bfloat16 [512, 2048], replicated, may hold values from -0.25 to 0.25
- w_out: bfloat16 [512, 512], replicated, may hold values from -0.25 to 0.25
- out_grad: bfloat16 [4096, 512], P(('rows', 'rep')), may hold values from -6 to 6
Outputs:
- new_hot_table: float32 [128, 512], replicated
- new_hot_accum: float32 [128], replicated
- new_cold_table: float32 [2048, 512], P('rows')
- new_cold_accum: float32 [2048], P('rows')
Inputs may be any that keep to these rules, and one draw needn't show every extreme that they name: `event_slots`: rows of the lookup buffer: the 128 hot rows, then 2 slots for each of the 8 owners; an event names slot k of owner j only if k is below that device's fetch_counts for j. `fetch_rows`: rows local to the owner's shard, distinct within one owner's 2 slots of one device; slots at or past the count are padding. `fetch_counts`: some owner is asked for 2 rows by every device.
All inputs are finite; a program needn't handle non-finite values.
Results may differ from a plain program's by a relative error of at most 0.0065.
Values sent between devices are 32-bit elements; how exact they have to be, the bound alone decides.
No kernel may reach another device: no remote copies, remote signals or barrier semaphores. Data moves between devices by JAX's collectives and lax.ppermute only.
A program may use at most 64 MiB of HBM per device.

v0:
```python
import jax
import jax.numpy as jnp
from jax import lax
from jax.sharding import PartitionSpec as P

HEAD = 128


STEP_RATE = 0.5


def hstu_layer(looked_up, ln_gain, ln_bias, w_in, w_out):
    seq_rows = looked_up.shape[0]
    inner = w_out.shape[0]
    n_heads = inner // HEAD
    row_mean = jnp.mean(looked_up, axis=1, keepdims=True)
    centered = looked_up - row_mean
    row_var = jnp.mean(centered * centered, axis=1, keepdims=True)
    normed = (centered * lax.rsqrt(row_var + 1e-05) * ln_gain + ln_bias).astype(jnp.bfloat16)
    projected = jax.nn.silu(jnp.dot(normed, w_in, preferred_element_type=jnp.float32)).astype(
        jnp.bfloat16
    )
    gates_u, values_v, queries, keys_k = jnp.split(projected, 4, axis=1)
    head_shape = (seq_rows, n_heads, HEAD)
    scores = jnp.einsum(
        "qhd,khd->hqk",
        queries.reshape(head_shape),
        keys_k.reshape(head_shape),
        preferred_element_type=jnp.float32,
    ) * HEAD ** (-0.5)
    causal = (
        lax.broadcasted_iota(jnp.int32, (seq_rows, seq_rows), 0)
        >= lax.broadcasted_iota(jnp.int32, (seq_rows, seq_rows), 1)
    ).astype(jnp.float32)
    attention = (jax.nn.silu(scores) * causal * (1.0 / seq_rows)).astype(jnp.bfloat16)
    mixed_val = jnp.einsum(
        "hqk,khd->qhd", attention, values_v.reshape(head_shape), preferred_element_type=jnp.float32
    ).reshape(seq_rows, inner)
    mixed_mean = jnp.mean(mixed_val, axis=1, keepdims=True)
    mixed_cent = mixed_val - mixed_mean
    mixed_var = jnp.mean(mixed_cent * mixed_cent, axis=1, keepdims=True)
    gated_val = (mixed_cent * lax.rsqrt(mixed_var + 1e-06) * gates_u.astype(jnp.float32)).astype(
        jnp.bfloat16
    )
    layer_out = looked_up + jnp.dot(gated_val, w_out, preferred_element_type=jnp.float32)
    return layer_out.astype(jnp.bfloat16)


def adagrad(table_rows, accum_rows, grad_rows):
    new_accum = accum_rows + jnp.mean(grad_rows * grad_rows, axis=1)
    return (table_rows - STEP_RATE * grad_rows * lax.rsqrt(new_accum)[:, None], new_accum)


def on_device(
    event_slots,
    fetch_rows,
    fetch_counts,
    hot_table,
    hot_accum,
    cold_table,
    cold_accum,
    ln_gain,
    ln_bias,
    w_in,
    w_out,
    out_grad,
):
    owner_count = lax.axis_size("rows")
    per_owner = fetch_rows.shape[1] // owner_count
    hot_rows, feature_width = hot_table.shape
    rows_shard = cold_table.shape[0]
    wanted_rows = fetch_rows.reshape(owner_count, per_owner)
    live_mask = (
        lax.broadcasted_iota(jnp.int32, (owner_count, per_owner), 1)
        < fetch_counts.reshape(owner_count, 1)
    ).astype(jnp.float32)[:, :, None]
    asked_rows = lax.all_to_all(wanted_rows, "rows", split_axis=0, concat_axis=0, tiled=True)
    found = cold_table[asked_rows]
    fetched = lax.all_to_all(found, "rows", split_axis=0, concat_axis=0, tiled=True)
    buffer = jnp.concatenate(
        [hot_table, (fetched * live_mask).reshape(owner_count * per_owner, feature_width)], axis=0
    )
    event_rows = event_slots.reshape(-1)
    looked_up = buffer[event_rows]

    def forward(lookup_rows):
        return hstu_layer(lookup_rows, ln_gain, ln_bias, w_in, w_out)

    _, backward = jax.vjp(forward, looked_up)
    (d_lookup,) = backward(out_grad)
    buffer_grad = jax.ops.segment_sum(
        d_lookup, event_rows, num_segments=hot_rows + owner_count * per_owner
    )
    returned = buffer_grad[hot_rows:].reshape(owner_count, per_owner, feature_width) * live_mask
    arrived = lax.all_to_all(returned, "rows", split_axis=0, concat_axis=0, tiled=True)
    cold_grad = jax.ops.segment_sum(
        arrived.reshape(-1, feature_width), asked_rows.reshape(-1), num_segments=rows_shard
    )
    hot_grad = buffer_grad[:hot_rows]
    group_sum = lax.psum(hot_grad, "rep")
    my_share = lax.psum_scatter(group_sum, "rows", scatter_dimension=0, tiled=True)
    span_rows = my_share.shape[0]
    first_row = lax.axis_index("rows") * span_rows
    own_rows = lax.dynamic_slice_in_dim(hot_table, first_row, span_rows, 0)
    own_accum = lax.dynamic_slice_in_dim(hot_accum, first_row, span_rows, 0)
    part_rows, part_accum = adagrad(own_rows, own_accum, my_share)
    new_hot_table, new_hot_accum = (
        lax.all_gather(part_rows, "rows", axis=0, tiled=True),
        lax.all_gather(part_accum, "rows", axis=0, tiled=True),
    )
    summed_cold = lax.psum(cold_grad, "rep")
    new_cold_table, new_cold_accum = adagrad(cold_table, cold_accum, summed_cold)
    return (new_hot_table, new_hot_accum, new_cold_table, new_cold_accum)


def solution(mesh):
    return jax.shard_map(
        on_device,
        mesh=mesh,
        in_specs=(
            P(("rows", "rep"), None),
            P(("rows", "rep"), None),
            P(("rows", "rep"), None),
            P(),
            P(),
            P("rows", None),
            P("rows"),
            P(),
            P(),
            P(),
            P(),
            P(("rows", "rep"), None),
        ),
        out_specs=(P(), P(), P("rows", None), P("rows")),
        check_vma=False,
    )
```

profile of v0, /device:TPU:0, one launch (start us, length us, event | category | flops | bytes accessed | tf_op | source)
XLA Modules:
  0.0 198.6 jit_solution(12410957981415220685)
XLA Ops:
  8.5 1.4 reduce.10
  10.6 7.3 %all-to-all-start = ((s32[8,1,2]{2,1,0:T(1,128)}), s32[8,1,2]{2,1,0:T(1,128)S(1)}, u32[]{:S(2)}, u32[]{:S(2)}) async-start(s32[8,1,2]{2,1,0:T(1,128)} %bitcast.1), calls=%async_computation | async-start | bytes 8192 | tf_op jit(solution)/shard_map/all_to_all | solution.py:77
  20.0 4.4 %all-to-all-done = s32[8,1,2]{2,1,0:T(1,128)S(1)} async-done(((s32[8,1,2]{2,1,0:T(1,128)}), s32[8,1,2]{2,1,0:T(1,128)S(1)}, u32[]{:S(2)}, u32[]{:S(2)}) %all-to-all-start) | async-done | bytes 96 | tf_op jit(solution)/shard_map/all_to_all | solution.py:77
  24.6 1.6 gather_fusion
  26.9 3.3 %all-to-all-start.1 = ((f32[8,2,512]{2,1,0:T(2,128)}), f32[8,2,512]{2,1,0:T(2,128)S(1)}, u32[]{:S(2)}, u32[]{:S(2)}) async-start(f32[8,2,512]{2,1,0:T(2,128)} %reshape.204), calls=%async_computation.1 | async-start | bytes 65536 | tf_op jit(solution)/shard_map/all_to_all | solution.py:79
  30.3 6.6 %all-to-all-done.1 = f32[8,2,512]{2,1,0:T(2,128)S(1)} async-done(((f32[8,2,512]{2,1,0:T(2,128)}), f32[8,2,512]{2,1,0:T(2,128)S(1)}, u32[]{:S(2)}, u32[]{:S(2)}) %all-to-all-start.1) | async-done | bytes 32800 | tf_op jit(solution)/shard_map/all_to_all | solution.py:79
  37.0 1.0 pad_maximum_fusion
  38.0 0.8 gather_fusion.1
  39.1 1.5 multiply_convert_fusion
  42.8 1.5 multiply_reduce_fusion.2
  44.3 1.7 fusion.52
  47.4 2.2 %multiply_reduce_fusion.1 = (f32[128]{0:T(128)S(1)}, f32[128,512]{1,0:T(8,128)S(1)}) fusion(f32[128,512]{1,0:T(8,128)S(1)} %gather_fusion.1, f32[128]{0:T(128)S(1)} %broadcast_multiply_fusion.3, f32[512]{0:T(512)S(1)} %copy-done.12, bf16[512,2048]{1,0:T(8,128)(2,1)S(1)} %copy-done, f32[128,2048]{1,0:T(8,128)} %get-tuple-element.19, ...), kind=kOutput, calls=%fused_computation.49 | convolution fusion | flops 273284992 | bytes 4197376 | tf_op jit(solution)/shard_map/transpose(jvp())/dot_general | solution.py:20
  49.9 1.6 scatter_custom_fusion
  52.2 3.5 %all-to-all-start.2 = ((f32[8,2,512]{2,1,0:T(2,128)}), f32[8,2,512]{2,1,0:T(2,128)S(1)}, u32[]{:S(2)}, u32[]{:S(2)}) async-start(f32[8,2,512]{2,1,0:T(2,128)} %broadcast_multiply_fusion), calls=%async_computation.2 | async-start | bytes 65536 | tf_op jit(solution)/shard_map/all_to_all | solution.py:95
  56.5 5.8 %all-to-all-done.2 = f32[8,2,512]{2,1,0:T(2,128)S(1)} async-done(((f32[8,2,512]{2,1,0:T(2,128)}), f32[8,2,512]{2,1,0:T(2,128)S(1)}, u32[]{:S(2)}, u32[]{:S(2)}) %all-to-all-start.2) | async-done | bytes 32800 | tf_op jit(solution)/shard_map/all_to_all | solution.py:95
  62.4 1.5 scatter_custom_fusion.1
  65.9 28.9 %all-reduce.3.cloned.1.call-done = f32[256,512]{1,0:T(8,128)} async-done(((f32[256,512]{1,0:T(8,128)}), f32[256,512]{1,0:T(8,128)}) %all-reduce.3.cloned.1.call-update) | async-done | bytes 524304 | tf_op jit(solution)/shard_map/psum | solution.py:111
  94.8 1.2 multiply_reduce_fusion
  96.5 1.9 multiply_subtract_fusion
  98.5 29.3 %reduce-scatter.2.cloned.1.call-done = f32[16,512]{1,0:T(8,128)} async-done(((f32[128,512]{1,0:T(8,128)}), f32[16,512]{1,0:T(8,128)}) %reduce-scatter.2.cloned.1.call-update) | async-done | bytes 32784 | tf_op jit(solution)/shard_map/reduce_scatter | solution.py:101
  127.7 10.8 %psum.16 = f32[16,512]{1,0:T(8,128)S(1)} all-reduce(f32[16,512]{1,0:T(8,128)} %reduce-scatter.2.cloned.1.call-done), channel_id=1, replica_groups=mesh['rows'=8,'rep'=4] {'rep'}, use_global_device_ids=true, to_apply=%region_9.10 | all-reduce | flops 8192 | bytes 65536 | tf_op jit(solution)/shard_map/psum | solution.py:100
  138.8 0.8 multiply_subtract_fusion.1
  139.7 19.9 %all-reduce = f32[128]{0:T(128)} all-reduce(f32[128]{0:T(128)S(1)} %get-tuple-element.14), channel_id=1, replica_groups=mesh['rows'=8,'rep'=4] {'rows'}, use_global_device_ids=true, to_apply=%add | all-reduce | flops 128 | bytes 1024
  159.6 30.8 %all_gather.6 = f32[128,512]{1,0:T(8,128)S(1)} all-gather(f32[16,512]{1,0:T(8,128)S(1)} %multiply_subtract_fusion.1), channel_id=1, replica_groups=mesh['rows'=8,'rep'=4] {'rows'}, dimensions={0}, use_global_device_ids=true | all-gather | bytes 294912 | tf_op jit(solution)/shard_map/all_gather | solution.py:108
  (84 shorter events, 12.7 us)
Async XLA Ops:
  8.0 31.0 %copy-start = (bf16[512,2048]{1,0:T(8,128)(2,1)S(1)}, bf16[512,2048]{1,0:T(8,128)(2,1)}, u32[]{:S(2)}) copy-start(bf16[512,2048]{1,0:T(8,128)(2,1)} %param.21) | copy-start | bytes 6291460
  10.6 13.7 %all-to-all-start = ((s32[8,1,2]{2,1,0:T(1,128)}), s32[8,1,2]{2,1,0:T(1,128)S(1)}, u32[]{:S(2)}, u32[]{:S(2)}) async-start(s32[8,1,2]{2,1,0:T(1,128)} %bitcast.1), calls=%async_computation | async-start | bytes 8192 | tf_op jit(solution)/shard_map/all_to_all | solution.py:77
  17.9 21.1 %copy-start.11 = (f32[512]{0:T(512)S(1)}, f32[512]{0:T(512)}, u32[]{:S(2)}) copy-start(f32[512]{0:T(512)} %param.20) | copy-start | bytes 6148
  17.9 21.1 %copy-start.12 = (f32[512]{0:T(512)S(1)}, f32[512]{0:T(512)}, u32[]{:S(2)}) copy-start(f32[512]{0:T(512)} %param.19) | copy-start | bytes 6148
  26.9 10.0 %all-to-all-start.1 = ((f32[8,2,512]{2,1,0:T(2,128)}), f32[8,2,512]{2,1,0:T(2,128)S(1)}, u32[]{:S(2)}, u32[]{:S(2)}) async-start(f32[8,2,512]{2,1,0:T(2,128)} %reshape.204), calls=%async_computation.1 | async-start | bytes 65536 | tf_op jit(solution)/shard_map/all_to_all | solution.py:79
  40.6 0.8 copy-start.2
  40.6 2.1 %copy-start.3 = (bf16[128,512]{1,0:T(8,128)(2,1)S(1)}, bf16[128,512]{1,0:T(8,128)(2,1)}, u32[]{:S(2)}) copy-start(bf16[128,512]{1,0:T(8,128)(2,1)} %param.23) | copy-start | bytes 393220
  41.4 2.9 %copy-start.6 = (bf16[16,4,8,128]{3,2,1,0:T(8,128)(2,1)}, bf16[16,4,8,128]{3,2,1,0:T(8,128)(2,1)S(1)}, u32[]{:S(2)}) copy-start(bf16[16,4,8,128]{3,2,1,0:T(8,128)(2,1)S(1)} %get-tuple-element.11) | copy-start | bytes 393220
  41.9 0.7 copy-start.4
  42.7 3.3 %copy-start.5 = (f32[4,128,128]{2,1,0:T(8,128)S(1)}, f32[4,128,128]{2,1,0:T(8,128)}, u32[]{:S(2)}) copy-start(f32[4,128,128]{2,1,0:T(8,128)} %copy-done.4) | copy-start | bytes 786436
  42.7 3.6 %copy-start.8 = (f32[128,128]{1,0:T(8,128)S(1)}, f32[128,128]{1,0:T(8,128)}, u32[]{:S(2)}) copy-start(f32[128,128]{1,0:T(8,128)} %fusion.42) | copy-start | bytes 196612
  44.3 2.1 %copy-start.7 = (bf16[16,4,8,128]{3,2,1,0:T(8,128)(2,1)S(1)}, bf16[16,4,8,128]{3,2,1,0:T(8,128)(2,1)}, u32[]{:S(2)}) copy-start(bf16[16,4,8,128]{3,2,1,0:T(8,128)(2,1)} %copy-done.6) | copy-start | bytes 393220
  49.6 14.3 %copy-start.13 = (u32[32]{0:T(128)S(1)}, u32[32]{0:T(128)}, u32[]{:S(2)}) copy-start(u32[32]{0:T(128)} %constant.60) | copy-start | bytes 388
  49.6 46.3 %copy-start.9 = (f32[256]{0:T(256)S(1)}, f32[256]{0:T(256)}, u32[]{:S(2)}) copy-start(f32[256]{0:T(256)} %param.18) | copy-start | bytes 3076
  49.6 46.9 %copy-start.1 = (f32[256,512]{1,0:T(8,128)S(1)}, f32[256,512]{1,0:T(8,128)}, u32[]{:S(2)}) copy-start(f32[256,512]{1,0:T(8,128)} %param.17) | copy-start | bytes 1572868
  52.2 86.4 %copy-start.10 = (f32[128]{0:T(128)S(1)}, f32[128]{0:T(128)}, u32[]{:S(2)}) copy-start(f32[128]{0:T(128)} %param.16) | copy-start | bytes 1540
  52.2 10.1 %all-to-all-start.2 = ((f32[8,2,512]{2,1,0:T(2,128)}), f32[8,2,512]{2,1,0:T(2,128)S(1)}, u32[]{:S(2)}, u32[]{:S(2)}) async-start(f32[8,2,512]{2,1,0:T(2,128)} %broadcast_multiply_fusion), calls=%async_computation.2 | async-start | bytes 65536 | tf_op jit(solution)/shard_map/all_to_all | solution.py:95
  55.7 39.1 %all-reduce.3.cloned.1.call-start = ((), (), s32[]{:S(2)}) async-start(), calls=%async_computation.4 | async-start | bytes 1048576 | tf_op jit(solution)/shard_map/psum | solution.py:111
  63.9 63.9 %reduce-scatter.2.cloned.1.call-start = ((), (), s32[]{:S(2)}) async-start(), calls=%async_computation.5 | async-start | bytes 294912 | tf_op jit(solution)/shard_map/reduce_scatter | solution.py:101
Sparse Core Ops, SparseCore 0:
  64.0 30.7 all-reduce.2
Sparse Core Ops, SparseCore 1:
  68.2 59.4 reduce-scatter.1
where the time goes:
time: 199 us
  waiting for transfers between devices  75 us (38%)
  blocking collectives  61.5 us (31%)
  between operations  16.5 us (8%)
  other arithmetic  16.1 us (8%)
  starting transfers between devices  14.2 us (7%)
  local copies, waits for them, and re-layouts  8.5 us (4%)
  matrix products  6.7 us (3%)
    all_gather x1, blocking collectives, on_device(): lax.all_gather(part_rows, 'rows', axis=0, tiled=True)  30.8 us
    reduce_scatter x1, waiting for transfers between devices, on_device(): lax.psum_scatter(group_sum, 'rows', scatter_dimension=0, tiled=True)  29.3 us
    psum x1, waiting for transfers between devices, on_device(): summed_cold = lax.psum(cold_grad, 'rep')  28.9 us
    unnamed x1, blocking collectives  19.9 us
    psum x1, blocking collectives, on_device(): group_sum = lax.psum(hot_grad, 'rep')  10.8 us
    all_to_all x1, starting transfers between devices, on_device(): lax.all_to_all(wanted_rows, 'rows', split_axis=0, concat_axis=0, tiled=True)  7.31 us
    all_to_all x1, waiting for transfers between devices, on_device(): lax.all_to_all(found, 'rows', split_axis=0, concat_axis=0, tiled=True)  6.61 us
    all_to_all x1, waiting for transfers between devices, on_device(): lax.all_to_all(returned, 'rows', split_axis=0, concat_axis=0, tiled=True)  5.82 us
  transfers between devices with their start and end apart: 5, of which 5 were waited for; matrix products, arithmetic and copies ran while one was open for 4% of the time, Pallas kernels for 0%

commit v1 on v0

v1 whole, which is shorter than its diff:
```python
import functools

import jax
import jax.numpy as jnp
from jax import lax
from jax.experimental import pallas as pl
from jax.experimental.pallas import tpu as pltpu
from jax.sharding import PartitionSpec as P

HEAD = 128
STEP_RATE = 0.5
LANES = 128
SUBLANES = 8
ALL = ("rows", "rep")
F32 = jnp.float32
BF16 = jnp.bfloat16

VMEM = pl.BlockSpec(memory_space=pltpu.VMEM)
SMEM = pl.BlockSpec(memory_space=pltpu.SMEM)


def params(mib=24):
    return pltpu.CompilerParams(vmem_limit_bytes=mib << 20)


def dot(a, b, dims, precision=None):
    return lax.dot_general(
        a, b, (dims, ((), ())), preferred_element_type=F32, precision=precision
    )


NN = ((1,), (0,))
NT = ((1,), (1,))
TN = ((0,), (0,))


def loop(count, body):
    for i in range(count):
        body(i)


def gather_kernel(place_ref, asked_ref, table_ref, out_ref, rows_scr, *, n_rows, n_rep, slot):
    j = place_ref[0]
    p = place_ref[1]
    per_row = asked_ref.shape[1]
    shard = table_ref.shape[0]
    width = table_ref.shape[1]
    chunks = width // LANES

    def take(r):
        rows_scr[pl.ds(r * per_row, per_row), :] = asked_ref[r * n_rep + p]

    loop(n_rows, take)
    asked = rows_scr[...].reshape(n_rows, per_row * LANES) if per_row == 1 else None
    table = table_ref[...]
    for k in range(slot):
        at = j * slot + k
        if per_row == 1:
            lane = lax.broadcasted_iota(jnp.int32, (n_rows, LANES), 1)
            col = jnp.sum(jnp.where(lane == at, asked, 0), axis=1, keepdims=True)
        else:
            flat = rows_scr[...].reshape(n_rows, per_row, LANES)
            pos = lax.broadcasted_iota(jnp.int32, flat.shape, 1) * LANES + lax.broadcasted_iota(
                jnp.int32, flat.shape, 2
            )
            col = jnp.sum(jnp.sum(jnp.where(pos == at, flat, 0), axis=1), axis=1, keepdims=True)
        pick = (lax.broadcasted_iota(jnp.int32, (n_rows, shard), 1) == col).astype(F32)
        rows = dot(pick, table, NN, lax.Precision.HIGHEST)
        for c in range(chunks):
            out_ref[:, k * chunks + c, :] = rows[:, c * LANES : (c + 1) * LANES]


def layer_kernel(
    event_ref,
    count_ref,
    hot_ref,
    fetched_ref,
    gain_ref,
    bias_ref,
    w_in_ref,
    w_out_ref,
    grad_ref,
    out_ref,
    x_scr,
    *,
    n_dev,
    n_rep,
    slot,
):
    hot_rows, width = hot_ref.shape
    n_owner = fetched_ref.shape[0]
    chunks = width // LANES
    slots = x_scr.shape[0]
    seq = grad_ref.shape[0]
    inner = w_out_ref.shape[0]
    heads = inner // HEAD

    x_scr[0:hot_rows, :] = hot_ref[...]

    def place(j):
        for k in range(slot):
            live = (k < count_ref[0, j]).astype(F32)
            for c in range(chunks):
                x_scr[pl.ds(hot_rows + j * slot + k, 1), c * LANES : (c + 1) * LANES] = (
                    fetched_ref[j, pl.ds(k * chunks + c, 1), :] * live
                )

    loop(n_owner, place)

    x = x_scr[...]
    mean = jnp.mean(x, axis=1, keepdims=True)
    cent = x - mean
    var = jnp.mean(cent * cent, axis=1, keepdims=True)
    rstd = lax.rsqrt(var + 1e-05)
    xhat = cent * rstd
    gain = gain_ref[...]
    normed = (xhat * gain + bias_ref[...]).astype(BF16)

    pre = dot(normed, w_in_ref[...], NN)
    sig = jax.nn.sigmoid(pre)
    proj = (pre * sig).astype(BF16)
    dsilu = sig * (1.0 + pre * (1.0 - sig))

    event_row = event_ref[...]
    scatter = (
        lax.broadcasted_iota(jnp.int32, (slots, seq), 0) == jnp.broadcast_to(event_row, (slots, seq))
    ).astype(F32)
    scatter_b = scatter.astype(BF16)

    proj_ev = dot(scatter_b, proj, TN).astype(BF16)
    gates = proj_ev[:, 0:inner].astype(F32)

    scale = HEAD ** (-0.5)
    causal = (
        lax.broadcasted_iota(jnp.int32, (seq, seq), 0)
        >= lax.broadcasted_iota(jnp.int32, (seq, seq), 1)
    ).astype(F32) * (1.0 / seq)

    values, queries, keys, atts, dacts, mixeds = [], [], [], [], [], []
    for h in range(heads):
        lo = h * HEAD
        v = proj_ev[:, inner + lo : inner + lo + HEAD]
        q = proj_ev[:, 2 * inner + lo : 2 * inner + lo + HEAD]
        kk = proj_ev[:, 3 * inner + lo : 3 * inner + lo + HEAD]
        s = dot(q, kk, NT) * scale
        sg = jax.nn.sigmoid(s)
        a = (s * sg * causal).astype(BF16)
        dacts.append(sg * (1.0 + s * (1.0 - sg)) * causal)
        values.append(v)
        queries.append(q)
        keys.append(kk)
        atts.append(a)
        mixeds.append(dot(a, v, NN))
    mixed = jnp.concatenate(mixeds, axis=1)
    mmean = jnp.mean(mixed, axis=1, keepdims=True)
    mcent = mixed - mmean
    mvar = jnp.mean(mcent * mcent, axis=1, keepdims=True)
    mrstd = lax.rsqrt(mvar + 1e-06)
    y = mcent * mrstd

    grad = grad_ref[...]
    d_gated = dot(grad, w_out_ref[...], NT).astype(BF16).astype(F32)
    d_gates = (d_gated * y).astype(BF16)
    d_y = d_gated * gates
    d_mixed = mrstd * (
        d_y - jnp.mean(d_y, axis=1, keepdims=True) - y * jnp.mean(d_y * y, axis=1, keepdims=True)
    )
    d_mixed = d_mixed.astype(BF16)
    d_vs, d_qs, d_ks = [], [], []
    for h in range(heads):
        dm = d_mixed[:, h * HEAD : (h + 1) * HEAD]
        d_a = dot(dm, values[h], NT).astype(BF16).astype(F32)
        d_vs.append(dot(atts[h], dm, TN).astype(BF16))
        d_s = (d_a * dacts[h] * scale).astype(BF16)
        d_qs.append(dot(d_s, keys[h], NN).astype(BF16))
        d_ks.append(dot(d_s, queries[h], TN).astype(BF16))
    d_proj = jnp.concatenate([d_gates] + d_vs + d_qs + d_ks, axis=1)

    d_slot = dot(scatter_b, d_proj, NN)
    d_pre = (d_slot * dsilu).astype(BF16)
    d_normed = dot(d_pre, w_in_ref[...], NT)
    d_hat = d_normed * gain
    d_x = rstd * (
        d_hat
        - jnp.mean(d_hat, axis=1, keepdims=True)
        - xhat * jnp.mean(d_hat * xhat, axis=1, keepdims=True)
    )
    x_scr[...] = d_x + dot(scatter_b, grad, NN)

    units = hot_rows * chunks
    share = units // n_dev
    for g in range(hot_rows // SUBLANES):
        for c in range(chunks):
            first = (g * chunks + c) * SUBLANES
            tile = x_scr[g * SUBLANES : (g + 1) * SUBLANES, c * LANES : (c + 1) * LANES]
            if share >= SUBLANES:
                out_ref[first // share, first % share : first % share + SUBLANES, :] = tile
            else:
                for i in range(SUBLANES):
                    q = first + i
                    out_ref[q // share, q % share : q % share + 1, :] = tile[i : i + 1, :]

    def send(j):
        for k in range(slot):
            live = (k < count_ref[0, j]).astype(F32)
            for c in range(chunks):
                row = (
                    x_scr[pl.ds(hot_rows + j * slot + k, 1), c * LANES : (c + 1) * LANES] * live
                )
                for p in range(n_rep):
                    out_ref[j * n_rep + p, pl.ds(share + k * chunks + c, 1), :] = row

    loop(n_owner, send)


def sum_kernel(got_ref, out_ref, *, share):
    n_dev = out_ref.shape[0]
    total = got_ref[0, 0:share, :]
    for d in range(1, n_dev):
        total = total + got_ref[d, 0:share, :]
    for d in range(n_dev):
        out_ref[d] = total


def cold_kernel(place_ref, asked_ref, got_ref, table_ref, accum_ref, new_ref, new_accum_ref, *, slot, share):
    j = place_ref[0]
    n_dev, per_row, _ = asked_ref.shape
    shard, width = table_ref.shape
    chunks = width // LANES
    asked = asked_ref[...]
    pos = lax.broadcasted_iota(jnp.int32, asked.shape, 1) * LANES + lax.broadcasted_iota(
        jnp.int32, asked.shape, 2
    )
    picks = []
    for k in range(slot):
        hit = jnp.where(pos == j * slot + k, asked, 0)
        col = jnp.sum(jnp.sum(hit, axis=1), axis=1, keepdims=True)
        picks.append(
            (lax.broadcasted_iota(jnp.int32, (n_dev, shard), 1) == col).astype(F32)
        )
    grads = []
    for c in range(chunks):
        part = None
        for k in range(slot):
            rows = got_ref[:, share + k * chunks + c, :]
            one = dot(picks[k], rows, TN, lax.Precision.HIGHEST)
            part = one if part is None else part + one
        grads.append(part)
    total = grads[0] * grads[0]
    for g in grads[1:]:
        total = total + g * g
    mean_sq = jnp.sum(total, axis=1, keepdims=True) * (1.0 / width)
    wide = jnp.transpose(jnp.broadcast_to(mean_sq, (shard, LANES)))
    accum_row = accum_ref[...]
    new_accum_ref[...] = accum_row + wide[0:1, :]
    accum_col = jnp.transpose(jnp.broadcast_to(accum_row, (LANES, shard)))[:, 0:1]
    step = lax.rsqrt(accum_col + mean_sq) * STEP_RATE
    for c in range(chunks):
        cols = slice(c * LANES, (c + 1) * LANES)
        new_ref[:, cols] = table_ref[:, cols] - grads[c] * step


def hot_kernel(got_ref, table_ref, accum_ref, new_ref, new_accum_ref, g_scr):
    n_dev, share, _ = got_ref.shape
    rows, width = table_ref.shape
    chunks = width // LANES
    for g in range(rows // SUBLANES):
        for c in range(chunks):
            first = (g * chunks + c) * SUBLANES
            at = (slice(g * SUBLANES, (g + 1) * SUBLANES), slice(c * LANES, (c + 1) * LANES))
            if share >= SUBLANES:
                g_scr[at] = got_ref[first // share, first % share : first % share + SUBLANES, :]
            else:
                for i in range(SUBLANES):
                    q = first + i
                    g_scr[g * SUBLANES + i : g * SUBLANES + i + 1, at[1]] = got_ref[
                        q // share, q % share : q % share + 1, :
                    ]
    grad = g_scr[...]
    mean_sq = jnp.mean(grad * grad, axis=1, keepdims=True)
    wide = jnp.transpose(jnp.broadcast_to(mean_sq, (rows, LANES)))
    accum_row = accum_ref[...]
    new_accum_ref[...] = accum_row + wide[0:1, :]
    accum_col = jnp.transpose(jnp.broadcast_to(accum_row, (LANES, rows)))[:, 0:1]
    new_ref[...] = table_ref[...] - STEP_RATE * grad * lax.rsqrt(accum_col + mean_sq)


def on_device(
    event_slots,
    fetch_rows,
    fetch_counts,
    hot_table,
    hot_accum,
    cold_table,
    cold_accum,
    ln_gain,
    ln_bias,
    w_in,
    w_out,
    out_grad,
):
    n_rows = lax.axis_size("rows")
    n_rep = lax.axis_size("rep")
    n_dev = n_rows * n_rep
    slot = fetch_rows.shape[1] // n_rows
    hot_rows, width = hot_table.shape
    shard = cold_table.shape[0]
    chunks = width // LANES
    share = hot_rows * chunks // n_dev
    asks = fetch_rows.shape[1]
    per_row = -(-asks // LANES)
    place = jnp.stack([lax.axis_index("rows"), lax.axis_index("rep")]).astype(jnp.int32)

    mine = jnp.pad(fetch_rows, ((0, 0), (0, per_row * LANES - asks))).reshape(1, per_row, LANES)
    asked = lax.all_to_all(
        jnp.broadcast_to(mine, (n_dev, per_row, LANES)), ALL, 0, 0, tiled=True
    )
    found = pl.pallas_call(
        functools.partial(gather_kernel, n_rows=n_rows, n_rep=n_rep, slot=slot),
        out_shape=jax.ShapeDtypeStruct((n_rows, slot * chunks, LANES), F32),
        in_specs=[SMEM, VMEM, VMEM],
        out_specs=VMEM,
        scratch_shapes=[pltpu.VMEM((n_rows * per_row, LANES), jnp.int32)],
        compiler_params=params(),
        name="gather",
    )(place, asked, cold_table)
    fetched = lax.all_to_all(found, "rows", 0, 0, tiled=True)

    slots = hot_rows + n_rows * slot
    sent = pl.pallas_call(
        functools.partial(layer_kernel, n_dev=n_dev, n_rep=n_rep, slot=slot),
        out_shape=jax.ShapeDtypeStruct((n_dev, share + slot * chunks, LANES), F32),
        in_specs=[VMEM, SMEM] + [VMEM] * 7,
        out_specs=VMEM,
        scratch_shapes=[pltpu.VMEM((slots, width), F32)],
        compiler_params=params(40),
        name="layer",
    )(
        event_slots,
        fetch_counts,
        hot_table,
        fetched,
        ln_gain.reshape(1, width),
        ln_bias.reshape(1, width),
        w_in,
        w_out,
        out_grad,
    )
    got = lax.all_to_all(sent, ALL, 0, 0, tiled=True)

    summed = pl.pallas_call(
        functools.partial(sum_kernel, share=share),
        out_shape=jax.ShapeDtypeStruct((n_dev, share, LANES), F32),
        in_specs=[VMEM],
        out_specs=VMEM,
        compiler_params=params(),
        name="sum",
    )(got)
    hot_grad = lax.all_to_all(summed, ALL, 0, 0, tiled=True)

    new_cold_table, new_cold_accum = pl.pallas_call(
        functools.partial(cold_kernel, slot=slot, share=share),
        out_shape=(
            jax.ShapeDtypeStruct((shard, width), F32),
            jax.ShapeDtypeStruct((1, shard), F32),
        ),
        in_specs=[SMEM] + [VMEM] * 4,
        out_specs=(VMEM, VMEM),
        compiler_params=params(),
        name="cold",
    )(place, asked, got, cold_table, cold_accum.reshape(1, shard))

    new_hot_table, new_hot_accum = pl.pallas_call(
        hot_kernel,
        out_shape=(
            jax.ShapeDtypeStruct((hot_rows, width), F32),
            jax.ShapeDtypeStruct((1, hot_rows), F32),
        ),
        in_specs=[VMEM] * 3,
        out_specs=(VMEM, VMEM),
        scratch_shapes=[pltpu.VMEM((hot_rows, width), F32)],
        compiler_params=params(),
        name="hot",
    )(hot_grad, hot_table, hot_accum.reshape(1, hot_rows))
    return (
        new_hot_table,
        new_hot_accum.reshape(hot_rows),
        new_cold_table,
        new_cold_accum.reshape(shard),
    )


def solution(mesh):
    return jax.shard_map(
        on_device,
        mesh=mesh,
        in_specs=(
            P(ALL, None),
            P(ALL, None),
            P(ALL, None),
            P(),
            P(),
            P("rows", None),
            P("rows"),
            P(),
            P(),
            P(),
            P(),
            P(ALL, None),
        ),
        out_specs=(P(), P(), P("rows", None), P("rows")),
        check_vma=False,
    )
```

time: 199 us -> 69.5 us (0.35)
  waiting for transfers between devices: 75 us -> 14.9 us
  blocking collectives: 61.5 us -> 24.2 us
  other arithmetic: 16.1 us -> 0.08 us
  between operations: 16.5 us -> 0.71 us
  Pallas kernels: 0 us -> 9.78 us
  matrix products: 6.7 us -> 0 us
  starting transfers between devices: 14.2 us -> 9.91 us
    all_gather x1 -> x0, blocking collectives: 30.8 us -> none  [on_device(): lax.all_gather(part_rows, 'rows', axis=0, tiled=True)]
    reduce_scatter x1 -> x0, waiting for transfers between devices: 29.3 us -> none  [on_device(): lax.psum_scatter(group_sum, 'rows', scatter_dimension=0, tiled=True)]
    psum x1 -> x0, waiting for transfers between devices: 28.9 us -> none  [on_device(): summed_cold = lax.psum(cold_grad, 'rep')]
    all_to_all x0 -> x2, blocking collectives: none -> 24.2 us  [the longest x1 15.1 us: on_device(): got = lax.all_to_all(sent, ALL, 0, 0, tiled=True)]
    unnamed x1 -> x0, blocking collectives: 19.9 us -> none
    psum x1 -> x0, blocking collectives: 10.8 us -> none  [on_device(): group_sum = lax.psum(hot_grad, 'rep')]
    pallas_call x0 -> x5, Pallas kernels: none -> 9.78 us  [the longest x1 4.16 us: on_device(): pl.pallas_call(functools.partial(layer_kernel, n_dev=n_dev, n_rep=n_rep,...]
    dot_general x9 -> x0, matrix products: 6.7 us -> none  [the longest x2 3.72 us: hstu_layer(): jnp.dot(normed, w_in, preferred_element_type=jnp.float32)]
  transfers between devices with their start and end apart: 5 -> 2, of which waited for: 5 -> 2; matrix products, arithmetic and copies ran while one was open for 4% -> 0% of each run, Pallas kernels for 0% -> 4%
where the time goes in v1:
time: 69.5 us; the launch traced here: 69 us
  blocking collectives  24.2 us (35%)
  waiting for transfers between devices  14.9 us (21%)
  starting transfers between devices  9.91 us (14%)
  Pallas kernels  9.78 us (14%)
  local copies, waits for them, and re-layouts  9.49 us (14%)
  between operations  0.71 us (1%)
    all_to_all x1, blocking collectives, on_device(): got = lax.all_to_all(sent, ALL, 0, 0, tiled=True)  15.1 us
    all_to_all x1, blocking collectives, on_device(): fetched = lax.all_to_all(found, 'rows', 0, 0, tiled=True)  9.06 us
    unnamed x26, local copies, waits for them, and re-layouts  8.22 us
    all_to_all x1, waiting for transfers between devices, on_device(): hot_grad = lax.all_to_all(summed, ALL, 0, 0, tiled=True)  7.83 us
    all_to_all x1, starting transfers between devices, on_device(): lax.all_to_all(jnp.broadcast_to(mine, (n_dev, per_row, LANES)), ALL, 0, 0...  7.33 us
    all_to_all x1, waiting for transfers between devices, on_device(): lax.all_to_all(jnp.broadcast_to(mine, (n_dev, per_row, LANES)), ALL, 0, 0...  7.02 us
    pallas_call x1, Pallas kernels, on_device(): pl.pallas_call(functools.partial(layer_kernel, n_dev=n_dev, n_rep=n_rep,...  4.16 us
    pallas_call x1, Pallas kernels, on_device(): pl.pallas_call(functools.partial(cold_kernel, slot=slot, share=share), ou...  2.72 us
  transfers between devices with their start and end apart: 2, of which 2 were waited for; matrix products, arithmetic and copies ran while one was open for 0% of the time, Pallas kernels for 4%

profile of v1, /device:TPU:0, one launch (start us, length us, event | category | flops | bytes accessed | tf_op | source)
XLA Modules:
  0.0 69.0 jit_solution(867054010898664009)
XLA Ops:
  0.6 0.7 pad_bitcast_fusion
  1.3 0.6 broadcast_in_dim.8
  1.9 7.3 %all-to-all-start = ((s32[32,1,128]{2,1,0:T(1,128)}), s32[32,1,128]{2,1,0:T(1,128)S(1)}, u32[]{:S(2)}, u32[]{:S(2)}) async-start(s32[32,1,128]{2,1,0:T(1,128)} %broadcast_in_dim.8), calls=%async_computation | async-start | bytes 32768 | tf_op jit(solution)/shard_map/all_to_all | solution.py:315
  9.2 0.1 pad_add_fusion.place_ref
  9.3 7.0 %all-to-all-done.asked_ref = s32[32,1,128]{2,1,0:T(1,128)S(1)} async-done(((s32[32,1,128]{2,1,0:T(1,128)}), s32[32,1,128]{2,1,0:T(1,128)S(1)}, u32[]{:S(2)}, u32[]{:S(2)}) %all-to-all-start) | async-done | bytes 16416 | tf_op jit(solution)/shard_map/all_to_all | solution.py:315
  16.3 1.0 %copy-done.1 = f32[256,512]{1,0:T(8,128)S(1)} copy-done((f32[256,512]{1,0:T(8,128)S(1)}, f32[256,512]{1,0:T(8,128)}, u32[]{:S(2)}) %copy-start.1) | copy-done | bytes 524312
  17.4 1.2 %gather.1 = f32[8,8,128]{2,1,0:T(8,128)S(1)} custom-call(s32[2]{0:T(128)S(1)} %pad_add_fusion.place_ref, s32[32,1,128]{2,1,0:T(1,128)S(1)} %all-to-all-done.asked_ref, f32[256,512]{1,0:T(8,128)S(1)} %copy-done.1), custom_call_target="tpu_custom_call" | custom-call | tf_op jit(solution)/shard_map/gather/pallas_call | solution.py:318
  18.5 9.1 %all_to_all.20.fetched_ref = f32[8,8,128]{2,1,0:T(8,128)S(1)} all-to-all(f32[8,8,128]{2,1,0:T(8,128)S(1)} %gather.1), channel_id=1, replica_groups=mesh['rows'=8,'rep'=4] {'rows'}, dimensions={0} | all-to-all | bytes 65536 | tf_op jit(solution)/shard_map/all_to_all | solution.py:327
  27.6 1.6 %copy-done = bf16[512,2048]{1,0:T(8,128)(2,1)S(1)} copy-done((bf16[512,2048]{1,0:T(8,128)(2,1)S(1)}, bf16[512,2048]{1,0:T(8,128)(2,1)}, u32[]{:S(2)}) %copy-start) | copy-done | bytes 2097176
  29.2 0.9 %copy-done.3 = f32[128,512]{1,0:T(8,128)S(1)} copy-done((f32[128,512]{1,0:T(8,128)S(1)}, f32[128,512]{1,0:T(8,128)}, u32[]{:S(2)}) %copy-start.3) | copy-done | bytes 262168
  30.2 1.0 %copy-done.5 = bf16[512,512]{1,0:T(8,128)(2,1)S(1)} copy-done((bf16[512,512]{1,0:T(8,128)(2,1)S(1)}, bf16[512,512]{1,0:T(8,128)(2,1)}, u32[]{:S(2)}) %copy-start.5) | copy-done | bytes 524312
  31.2 0.9 %copy-done.6 = bf16[128,512]{1,0:T(8,128)(2,1)S(1)} copy-done((bf16[128,512]{1,0:T(8,128)(2,1)S(1)}, bf16[128,512]{1,0:T(8,128)(2,1)}, u32[]{:S(2)}) %copy-start.6) | copy-done | bytes 131096
  32.1 0.7 copy-done.7
  32.8 0.7 copy-done.8
  33.5 0.7 copy-done.10
  34.1 0.7 copy-done.11
  34.8 4.2 %layer.1 = f32[32,24,128]{2,1,0:T(8,128)S(1)} custom-call(s32[1,128]{1,0:T(1,128)S(1)} %copy-done.10, s32[1,8]{1,0:T(1,128)S(1)} %copy-done.11, f32[128,512]{1,0:T(8,128)S(1)} %copy-done.3, f32[8,8,128]{2,1,0:T(8,128)S(1)} %all_to_all.20.fetched_ref, f32[1,512]{1,0:T(1,128)S(1)} %bitcast.10, f32[1,512]{1,0:T(1,128)S(1)} %bitcast.11, ...), custom_call_target="tpu_custom_call" | custom-call | tf_op jit(solution)/shard_map/layer/pallas_call | solution.py:330
  38.9 0.0 copy-start.4
  39.0 15.1 %all_to_all.21.got_ref = f32[32,24,128]{2,1,0:T(8,128)S(1)} all-to-all(f32[32,24,128]{2,1,0:T(8,128)S(1)} %layer.1), channel_id=1, replica_groups=mesh['rows'=8,'rep'=4] {'rows','rep'}, dimensions={0} | all-to-all | bytes 786432 | tf_op jit(solution)/shard_map/all_to_all | solution.py:349
  54.1 0.8 %sum.1 = f32[32,16,128]{2,1,0:T(8,128)} custom-call(f32[32,24,128]{2,1,0:T(8,128)S(1)} %all_to_all.21.got_ref), custom_call_target="tpu_custom_call" | custom-call | tf_op jit(solution)/shard_map/sum/pallas_call | solution.py:351
  54.8 2.6 %all-to-all-start.3 = ((f32[32,16,128]{2,1,0:T(8,128)}), f32[32,16,128]{2,1,0:T(8,128)S(1)}, u32[]{:S(2)}, u32[]{:S(2)}) async-start(f32[32,16,128]{2,1,0:T(8,128)} %sum.1), calls=%async_computation.3 | async-start | bytes 524288 | tf_op jit(solution)/shard_map/all_to_all | solution.py:359
  57.4 2.7 %cold.1 = (f32[256,512]{1,0:T(8,128)}, f32[1,256]{1,0:T(1,128)}) custom-call(s32[2]{0:T(128)S(1)} %pad_add_fusion.place_ref, s32[32,1,128]{2,1,0:T(1,128)S(1)} %all-to-all-done.asked_ref, f32[32,24,128]{2,1,0:T(8,128)S(1)} %all_to_all.21.got_ref, f32[256,512]{1,0:T(8,128)S(1)} %copy-done.2, f32[1,256]{1,0:T(1,128)S(1)} %bitcast.12), custom_call_target="tpu_custom_call" | custom-call | tf_op jit(solution)/shard_map/cold/pallas_call | solution.py:361
  60.1 7.8 %all-to-all-done.3.got_ref = f32[32,16,128]{2,1,0:T(8,128)S(1)} async-done(((f32[32,16,128]{2,1,0:T(8,128)}), f32[32,16,128]{2,1,0:T(8,128)S(1)}, u32[]{:S(2)}, u32[]{:S(2)}) %all-to-all-start.3) | async-done | bytes 262176 | tf_op jit(solution)/shard_map/all_to_all | solution.py:359
  68.0 1.0 %hot.1 = (f32[128,512]{1,0:T(8,128)}, f32[1,128]{1,0:T(1,128)}) custom-call(f32[32,16,128]{2,1,0:T(8,128)S(1)} %all-to-all-done.3.got_ref, f32[128,512]{1,0:T(8,128)S(1)} %copy-done.4, f32[1,128]{1,0:T(1,128)S(1)} %bitcast.13), custom_call_target="tpu_custom_call" | custom-call | tf_op jit(solution)/shard_map/hot/pallas_call | solution.py:373
  (16 shorter events, 0.0 us)
Async XLA Ops:
  1.9 14.4 %all-to-all-start = ((s32[32,1,128]{2,1,0:T(1,128)}), s32[32,1,128]{2,1,0:T(1,128)S(1)}, u32[]{:S(2)}, u32[]{:S(2)}) async-start(s32[32,1,128]{2,1,0:T(1,128)} %broadcast_in_dim.8), calls=%async_computation | async-start | bytes 32768 | tf_op jit(solution)/shard_map/all_to_all | solution.py:315
  16.3 1.0 %copy-start.1 = (f32[256,512]{1,0:T(8,128)S(1)}, f32[256,512]{1,0:T(8,128)}, u32[]{:S(2)}) copy-start(f32[256,512]{1,0:T(8,128)} %table_ref.5) | copy-start | bytes 1572868
  27.6 1.6 %copy-start = (bf16[512,2048]{1,0:T(8,128)(2,1)S(1)}, bf16[512,2048]{1,0:T(8,128)(2,1)}, u32[]{:S(2)}) copy-start(bf16[512,2048]{1,0:T(8,128)(2,1)} %w_in_ref.1) | copy-start | bytes 6291460
  29.2 0.9 %copy-start.3 = (f32[128,512]{1,0:T(8,128)S(1)}, f32[128,512]{1,0:T(8,128)}, u32[]{:S(2)}) copy-start(f32[128,512]{1,0:T(8,128)} %table_ref.4) | copy-start | bytes 786436
  30.2 1.0 %copy-start.5 = (bf16[512,512]{1,0:T(8,128)(2,1)S(1)}, bf16[512,512]{1,0:T(8,128)(2,1)}, u32[]{:S(2)}) copy-start(bf16[512,512]{1,0:T(8,128)(2,1)} %w_out_ref.1) | copy-start | bytes 1572868
  31.2 0.9 %copy-start.6 = (bf16[128,512]{1,0:T(8,128)(2,1)S(1)}, bf16[128,512]{1,0:T(8,128)(2,1)}, u32[]{:S(2)}) copy-start(bf16[128,512]{1,0:T(8,128)(2,1)} %grad_ref.1) | copy-start | bytes 393220
  32.1 0.7 copy-start.7
  32.8 0.7 copy-start.8
  33.5 0.7 copy-start.10
  34.1 0.7 copy-start.11
  34.8 22.6 %copy-start.2 = (f32[256,512]{1,0:T(8,128)S(1)}, f32[256,512]{1,0:T(8,128)}, u32[]{:S(2)}) copy-start(f32[256,512]{1,0:T(8,128)} %table_ref.5) | copy-start | bytes 1572868
  34.8 22.6 %copy-start.9 = (f32[256]{0:T(256)S(1)}, f32[256]{0:T(256)}, u32[]{:S(2)}) copy-start(f32[256]{0:T(256)} %param.18) | copy-start | bytes 3076
  38.9 29.0 %copy-start.4 = (f32[128,512]{1,0:T(8,128)S(1)}, f32[128,512]{1,0:T(8,128)}, u32[]{:S(2)}) copy-start(f32[128,512]{1,0:T(8,128)} %table_ref.4) | copy-start | bytes 786436
  39.0 29.0 %copy-start.12 = (f32[128]{0:T(128)S(1)}, f32[128]{0:T(128)}, u32[]{:S(2)}) copy-start(f32[128]{0:T(128)} %param.16) | copy-start | bytes 1540
  54.8 13.2 %all-to-all-start.3 = ((f32[32,16,128]{2,1,0:T(8,128)}), f32[32,16,128]{2,1,0:T(8,128)S(1)}, u32[]{:S(2)}, u32[]{:S(2)}) async-start(f32[32,16,128]{2,1,0:T(8,128)} %sum.1), calls=%async_computation.3 | async-start | bytes 524288 | tf_op jit(solution)/shard_map/all_to_all | solution.py:359

commit v2 on v1

v2 whole, which is shorter than its diff:
```python
import functools

import jax
import jax.numpy as jnp
from jax import lax
from jax.experimental import pallas as pl
from jax.experimental.pallas import tpu as pltpu
from jax.sharding import PartitionSpec as P

HEAD = 128
STEP_RATE = 0.5
LANES = 128
SUBLANES = 8
ALL = ("rows", "rep")
F32 = jnp.float32
BF16 = jnp.bfloat16

VMEM = pl.BlockSpec(memory_space=pltpu.VMEM)
ANY = pl.BlockSpec(memory_space=pl.ANY)


def params(mib=24):
    return pltpu.CompilerParams(vmem_limit_bytes=mib << 20)


def dot(a, b, dims, precision=None):
    return lax.dot_general(
        a, b, (dims, ((), ())), preferred_element_type=F32, precision=precision
    )


NN = ((1,), (0,))
NT = ((1,), (1,))
TN = ((0,), (0,))


def gather_kernel(asked_ref, table_ref, out_ref, rows_scr, *, n_rows, n_rep, slot):
    j = lax.axis_index("rows")
    p = lax.axis_index("rep")
    shard = table_ref.shape[0]
    width = table_ref.shape[1] // 3
    chunks = width // LANES

    for r in range(n_rows):
        rows_scr[r : r + 1, :] = asked_ref[r * n_rep + p]
    asked = rows_scr[...]
    pos = lax.broadcasted_iota(jnp.int32, asked.shape, 1)
    picks = []
    for k in range(slot):
        col = jnp.sum(jnp.where(pos == j * slot + k, asked, 0), axis=1, keepdims=True)
        picks.append((lax.broadcasted_iota(jnp.int32, (n_rows, shard), 1) == col).astype(F32))
    pick = jnp.concatenate(picks, axis=0).astype(BF16)
    rows = dot(pick, table_ref[...], NN)
    rows = rows[:, 0:width] + rows[:, width : 2 * width] + rows[:, 2 * width : 3 * width]
    for k in range(slot):
        for c in range(chunks):
            out_ref[:, k * chunks + c, :] = rows[
                k * n_rows : (k + 1) * n_rows, c * LANES : (c + 1) * LANES
            ]


def normalise(x, eps):
    cent = x - jnp.mean(x, axis=1, keepdims=True)
    rstd = lax.rsqrt(jnp.mean(cent * cent, axis=1, keepdims=True) + eps)
    return cent * rstd, rstd


def project(x_hat, gain, bias, w_in):
    pre = dot((x_hat * gain + bias).astype(BF16), w_in, NN)
    sig = jax.nn.sigmoid(pre)
    return (pre * sig).astype(BF16), sig * (1.0 + pre * (1.0 - sig))


def early_kernel(
    event_hbm,
    count_hbm,
    hot_hbm,
    gain_hbm,
    bias_hbm,
    w_in_hbm,
    w_out_hbm,
    grad_hbm,
    cold_hbm,
    w_in_ref,
    proj_ref,
    pick_ref,
    live_ref,
    gain_ref,
    bias_ref,
    parts_ref,
    gated_out,
    scatter_out,
    dsilu_out,
    hat_out,
    rstd_out,
    base_out,
    gated_ref,
    scatter_ref,
    dsilu_ref,
    hat_ref,
    rstd_ref,
    base_ref,
    event_scr,
    count_scr,
    hot_scr,
    w_out_scr,
    grad_scr,
    cold_scr,
    sems,
    out_sems,
    *,
    n_owner,
    slot,
):
    copies = [
        pltpu.make_async_copy(src, dst, sems.at[i])
        for i, (src, dst) in enumerate(
            (
                (cold_hbm, cold_scr),
                (event_hbm, event_scr),
                (count_hbm, count_scr),
                (hot_hbm, hot_scr),
                (gain_hbm, gain_ref),
                (bias_hbm, bias_ref),
                (grad_hbm, grad_scr),
                (w_out_hbm, w_out_scr),
                (w_in_hbm, w_in_ref),
            )
        )
    ]
    for copy in copies:
        copy.start()
    sends = {
        name: pltpu.make_async_copy(src, dst, out_sems.at[i])
        for i, (name, src, dst) in enumerate(
            (
                ("gated", gated_ref, gated_out),
                ("scatter", scatter_ref, scatter_out),
                ("dsilu", dsilu_ref, dsilu_out),
                ("hat", hat_ref, hat_out),
                ("rstd", rstd_ref, rstd_out),
                ("base", base_ref, base_out),
            )
        )
    }
    hot_rows, width = hot_scr.shape
    seq = grad_scr.shape[0]
    slots = scatter_ref.shape[0]
    fetched = slots - hot_rows

    copies[0].wait()
    cold = cold_scr[...]
    high = cold.astype(BF16)
    rest = cold - high.astype(F32)
    mid = rest.astype(BF16)
    parts_ref[:, 0:width] = high
    parts_ref[:, width : 2 * width] = mid
    parts_ref[:, 2 * width : 3 * width] = (rest - mid.astype(F32)).astype(BF16)

    copies[1].wait()
    copies[2].wait()
    event_row = event_scr[...]
    scatter = (
        lax.broadcasted_iota(jnp.int32, (slots, seq), 0) == jnp.broadcast_to(event_row, (slots, seq))
    ).astype(F32)
    scatter_ref[...] = scatter.astype(BF16)
    sends["scatter"].start()
    pick_ref[...] = jnp.transpose(scatter[hot_rows:slots, :]).astype(BF16)
    owner = lax.broadcasted_iota(jnp.int32, (fetched, n_owner), 0) // slot
    mine = owner == lax.broadcasted_iota(jnp.int32, (fetched, n_owner), 1)
    counts = jnp.broadcast_to(count_scr[...], (fetched, n_owner))
    count_col = jnp.sum(jnp.where(mine, counts, 0), axis=1, keepdims=True)
    turn = lax.broadcasted_iota(jnp.int32, (fetched, LANES), 0) % slot
    live_ref[...] = (turn < count_col).astype(F32)

    for i in (3, 4, 5):
        copies[i].wait()
    x_hat, rstd = normalise(hot_scr[...], 1e-05)
    hat_ref[...] = x_hat
    rstd_ref[...] = jnp.broadcast_to(rstd, (hot_rows, LANES))
    sends["hat"].start()
    sends["rstd"].start()

    copies[6].wait()
    grad = grad_scr[...]
    base_ref[...] = dot(scatter.astype(BF16), grad, NN)
    sends["base"].start()
    copies[7].wait()
    gated_ref[...] = dot(grad, w_out_scr[...], NT).astype(BF16)
    sends["gated"].start()
    copies[8].wait()
    proj, dsilu = project(x_hat, gain_ref[...], bias_ref[...], w_in_ref[...])
    dsilu_ref[...] = dsilu
    sends["dsilu"].start()
    proj_ref[...] = dot(scatter[0:hot_rows, :].astype(BF16), proj, TN).astype(BF16)
    for send in sends.values():
        send.wait()


def layer_kernel(
    fetched_ref,
    w_in_ref,
    proj_ref,
    pick_ref,
    live_ref,
    gain_ref,
    bias_ref,
    gated_hbm,
    scatter_hbm,
    dsilu_hbm,
    hat_hbm,
    rstd_hbm,
    base_hbm,
    out_ref,
    x_scr,
    g_scr,
    gated_ref,
    scatter_ref,
    dsilu_ref,
    hat_ref,
    rstd_ref,
    base_ref,
    sems,
    *,
    n_dev,
    n_rep,
    slot,
):
    copies = [
        pltpu.make_async_copy(src, dst, sems.at[i])
        for i, (src, dst) in enumerate(
            (
                (gated_hbm, gated_ref),
                (scatter_hbm, scatter_ref),
                (dsilu_hbm, dsilu_ref),
                (hat_hbm, hat_ref),
                (rstd_hbm, rstd_ref),
                (base_hbm, base_ref),
            )
        )
    ]
    for copy in copies:
        copy.start()
    hot_rows, width = hat_ref.shape
    n_owner = fetched_ref.shape[0]
    chunks = width // LANES
    slots = scatter_ref.shape[0]
    seq, inner = gated_ref.shape
    heads = inner // HEAD
    gain = gain_ref[...]

    for j in range(n_owner):
        for k in range(slot):
            for c in range(chunks):
                x_scr[j * slot + k : j * slot + k + 1, c * LANES : (c + 1) * LANES] = fetched_ref[
                    j, k * chunks + c : k * chunks + c + 1, :
                ]
    live = live_ref[:, 0:1]
    cold_hat, cold_rstd = normalise(x_scr[...] * live, 1e-05)
    cold_proj, cold_dsilu = project(cold_hat, gain, bias_ref[...], w_in_ref[...])
    proj_ev = (proj_ref[...].astype(F32) + dot(pick_ref[...], cold_proj, NN)).astype(BF16)
    gates = proj_ev[:, 0:inner].astype(F32)

    scale = HEAD ** (-0.5)
    causal = (
        lax.broadcasted_iota(jnp.int32, (seq, seq), 0)
        >= lax.broadcasted_iota(jnp.int32, (seq, seq), 1)
    ).astype(F32) * (1.0 / seq)

    values, queries, keys, atts, dacts, mixeds = [], [], [], [], [], []
    for h in range(heads):
        lo = h * HEAD
        v = proj_ev[:, inner + lo : inner + lo + HEAD]
        q = proj_ev[:, 2 * inner + lo : 2 * inner + lo + HEAD]
        kk = proj_ev[:, 3 * inner + lo : 3 * inner + lo + HEAD]
        s = dot(q, kk, NT) * scale
        sg = jax.nn.sigmoid(s)
        a = (s * sg * causal).astype(BF16)
        dacts.append(sg * (1.0 + s * (1.0 - sg)) * causal)
        values.append(v)
        queries.append(q)
        keys.append(kk)
        atts.append(a)
        mixeds.append(dot(a, v, NN))
    y, mrstd = normalise(jnp.concatenate(mixeds, axis=1), 1e-06)

    copies[0].wait()
    d_gated = gated_ref[...].astype(F32)
    d_gates = (d_gated * y).astype(BF16)
    d_y = d_gated * gates
    d_mixed = mrstd * (
        d_y - jnp.mean(d_y, axis=1, keepdims=True) - y * jnp.mean(d_y * y, axis=1, keepdims=True)
    )
    d_mixed = d_mixed.astype(BF16)
    d_vs, d_qs, d_ks = [], [], []
    for h in range(heads):
        dm = d_mixed[:, h * HEAD : (h + 1) * HEAD]
        d_a = dot(dm, values[h], NT).astype(BF16).astype(F32)
        d_vs.append(dot(atts[h], dm, TN).astype(BF16))
        d_s = (d_a * dacts[h] * scale).astype(BF16)
        d_qs.append(dot(d_s, keys[h], NN).astype(BF16))
        d_ks.append(dot(d_s, queries[h], TN).astype(BF16))
    d_proj = jnp.concatenate([d_gates] + d_vs + d_qs + d_ks, axis=1)

    for copy in copies[1:]:
        copy.wait()
    d_slot = dot(scatter_ref[...], d_proj, NN)
    d_pre = jnp.concatenate(
        [d_slot[0:hot_rows] * dsilu_ref[...], d_slot[hot_rows:slots] * cold_dsilu], axis=0
    ).astype(BF16)
    d_hat = dot(d_pre, w_in_ref[...], NT) * gain

    def back(d, x_hat, rstd):
        return rstd * (
            d - jnp.mean(d, axis=1, keepdims=True) - x_hat * jnp.mean(d * x_hat, axis=1, keepdims=True)
        )

    hot = back(d_hat[0:hot_rows], hat_ref[...], rstd_ref[:, 0:1]) + base_ref[0:hot_rows, :]
    cold = back(d_hat[hot_rows:slots], cold_hat, cold_rstd) + base_ref[hot_rows:slots, :]
    x_scr[...] = cold * live

    units = hot_rows * chunks
    share = units // n_dev
    if share < SUBLANES:
        g_scr[...] = hot
    for g in range(hot_rows // SUBLANES):
        for c in range(chunks):
            first = (g * chunks + c) * SUBLANES
            at = (slice(g * SUBLANES, (g + 1) * SUBLANES), slice(c * LANES, (c + 1) * LANES))
            if share >= SUBLANES:
                out_ref[first // share, first % share : first % share + SUBLANES, :] = hot[at]
            else:
                for i in range(SUBLANES):
                    q = first + i
                    row = g * SUBLANES + i
                    out_ref[q // share, q % share : q % share + 1, :] = g_scr[row : row + 1, at[1]]

    for j in range(n_owner):
        for k in range(slot):
            for c in range(chunks):
                at = j * slot + k
                row = x_scr[at : at + 1, c * LANES : (c + 1) * LANES]
                to = share + k * chunks + c
                for p in range(n_rep):
                    out_ref[j * n_rep + p, to : to + 1, :] = row


def sum_kernel(got_ref, out_ref, *, share):
    n_dev = out_ref.shape[0]
    total = got_ref[0, 0:share, :]
    for d in range(1, n_dev):
        total = total + got_ref[d, 0:share, :]
    for d in range(n_dev):
        out_ref[d] = total


def cold_kernel(asked_ref, got_ref, table_ref, accum_ref, new_ref, new_accum_ref, *, slot, share):
    j = lax.axis_index("rows")
    n_dev = asked_ref.shape[0]
    shard, width = table_ref.shape
    chunks = width // LANES
    asked = asked_ref[:, 0, :]
    pos = lax.broadcasted_iota(jnp.int32, asked.shape, 1)
    picks = []
    for k in range(slot):
        col = jnp.sum(jnp.where(pos == j * slot + k, asked, 0), axis=1, keepdims=True)
        picks.append(
            (lax.broadcasted_iota(jnp.int32, (n_dev, shard), 1) == col).astype(F32)
        )
    grads = []
    for c in range(chunks):
        part = None
        for k in range(slot):
            rows = got_ref[:, share + k * chunks + c, :]
            one = dot(picks[k], rows, TN, lax.Precision.HIGHEST)
            part = one if part is None else part + one
        grads.append(part)
    total = grads[0] * grads[0]
    for g in grads[1:]:
        total = total + g * g
    mean_sq = jnp.sum(total, axis=1, keepdims=True) * (1.0 / width)
    wide = jnp.transpose(jnp.broadcast_to(mean_sq, (shard, LANES)))
    accum_row = accum_ref[...]
    new_accum_ref[...] = accum_row + wide[0:1, :]
    accum_col = jnp.transpose(jnp.broadcast_to(accum_row, (LANES, shard)))[:, 0:1]
    step = lax.rsqrt(accum_col + mean_sq) * STEP_RATE
    for c in range(chunks):
        cols = slice(c * LANES, (c + 1) * LANES)
        new_ref[:, cols] = table_ref[:, cols] - grads[c] * step


def hot_kernel(got_ref, table_ref, accum_ref, new_ref, new_accum_ref, g_scr):
    n_dev, share, _ = got_ref.shape
    rows, width = table_ref.shape
    chunks = width // LANES
    for g in range(rows // SUBLANES):
        for c in range(chunks):
            first = (g * chunks + c) * SUBLANES
            at = (slice(g * SUBLANES, (g + 1) * SUBLANES), slice(c * LANES, (c + 1) * LANES))
            if share >= SUBLANES:
                g_scr[at] = got_ref[first // share, first % share : first % share + SUBLANES, :]
            else:
                for i in range(SUBLANES):
                    q = first + i
                    g_scr[g * SUBLANES + i : g * SUBLANES + i + 1, at[1]] = got_ref[
                        q // share, q % share : q % share + 1, :
                    ]
    grad = g_scr[...]
    mean_sq = jnp.mean(grad * grad, axis=1, keepdims=True)
    wide = jnp.transpose(jnp.broadcast_to(mean_sq, (rows, LANES)))
    accum_row = accum_ref[...]
    new_accum_ref[...] = accum_row + wide[0:1, :]
    accum_col = jnp.transpose(jnp.broadcast_to(accum_row, (LANES, rows)))[:, 0:1]
    new_ref[...] = table_ref[...] - STEP_RATE * grad * lax.rsqrt(accum_col + mean_sq)


def on_device(
    event_slots,
    fetch_rows,
    fetch_counts,
    hot_table,
    hot_accum,
    cold_table,
    cold_accum,
    ln_gain,
    ln_bias,
    w_in,
    w_out,
    out_grad,
):
    n_rows = lax.axis_size("rows")
    n_rep = lax.axis_size("rep")
    n_dev = n_rows * n_rep
    slot = fetch_rows.shape[1] // n_rows
    hot_rows, width = hot_table.shape
    shard = cold_table.shape[0]
    chunks = width // LANES
    share = hot_rows * chunks // n_dev
    asks = fetch_rows.shape[1]
    slots = hot_rows + asks
    seq, inner = out_grad.shape[0], w_out.shape[0]

    with jax.named_scope("asks"):
        asked = lax.all_to_all(
            jnp.broadcast_to(fetch_rows.reshape(1, 1, asks), (n_dev, 1, asks)), ALL, 0, 0, tiled=True
        )
    late = (
        ((seq, inner), BF16),
        ((slots, seq), BF16),
        ((hot_rows, w_in.shape[1]), F32),
        ((hot_rows, width), F32),
        ((hot_rows, LANES), F32),
        ((slots, width), F32),
    )
    early = pl.pallas_call(
        functools.partial(early_kernel, n_owner=n_rows, slot=slot),
        out_shape=(
            pltpu.VMEM(w_in.shape, BF16),
            pltpu.VMEM((seq, w_in.shape[1]), BF16),
            pltpu.VMEM((seq, asks), BF16),
            pltpu.VMEM((asks, LANES), F32),
            pltpu.VMEM((1, width), F32),
            pltpu.VMEM((1, width), F32),
            pltpu.VMEM((shard, 3 * width), BF16),
        )
        + tuple(pltpu.HBM(*x) for x in late),
        in_specs=[ANY] * 9,
        out_specs=(VMEM,) * 7 + (ANY,) * 6,
        scratch_shapes=[pltpu.VMEM(*x) for x in late]
        + [
            pltpu.VMEM(event_slots.shape, jnp.int32),
            pltpu.VMEM(fetch_counts.shape, jnp.int32),
            pltpu.VMEM((hot_rows, width), F32),
            pltpu.VMEM(w_out.shape, BF16),
            pltpu.VMEM(out_grad.shape, BF16),
            pltpu.VMEM((shard, width), F32),
            pltpu.SemaphoreType.DMA((9,)),
            pltpu.SemaphoreType.DMA((6,)),
        ],
        compiler_params=params(),
        cost_estimate=pl.CostEstimate(flops=4 * 10**9, bytes_accessed=8 << 20, transcendentals=0),
        name="early",
    )(
        *(
            pltpu.with_memory_space_constraint(x, pltpu.HBM)
            for x in (
                event_slots,
                fetch_counts,
                hot_table,
                ln_gain.reshape(1, width),
                ln_bias.reshape(1, width),
                w_in,
                w_out,
                out_grad,
                cold_table,
            )
        )
    )
    early = [
        pltpu.with_memory_space_constraint(x, pltpu.VMEM if i < 7 else pltpu.HBM)
        for i, x in enumerate(early)
    ]
    found = pl.pallas_call(
        functools.partial(gather_kernel, n_rows=n_rows, n_rep=n_rep, slot=slot),
        out_shape=jax.ShapeDtypeStruct((n_rows, slot * chunks, LANES), F32),
        in_specs=[VMEM, VMEM],
        out_specs=VMEM,
        scratch_shapes=[pltpu.VMEM((n_rows, asks), jnp.int32)],
        compiler_params=params(),
        name="gather",
    )(asked, early[6])
    fetched = lax.all_to_all(found, "rows", 0, 0, tiled=True)

    sent = pl.pallas_call(
        functools.partial(layer_kernel, n_dev=n_dev, n_rep=n_rep, slot=slot),
        out_shape=jax.ShapeDtypeStruct((n_dev, share + slot * chunks, LANES), F32),
        in_specs=[VMEM] * 7 + [ANY] * 6,
        out_specs=VMEM,
        scratch_shapes=[pltpu.VMEM((asks, width), F32), pltpu.VMEM((hot_rows, width), F32)]
        + [pltpu.VMEM(*x) for x in late]
        + [pltpu.SemaphoreType.DMA((6,))],
        compiler_params=params(),
        name="layer",
    )(fetched, *early[:6], *early[7:])
    got = lax.all_to_all(sent, ALL, 0, 0, tiled=True)

    summed = pl.pallas_call(
        functools.partial(sum_kernel, share=share),
        out_shape=jax.ShapeDtypeStruct((n_dev, share, LANES), F32),
        in_specs=[VMEM],
        out_specs=VMEM,
        compiler_params=params(),
        name="sum",
    )(got)
    hot_grad = lax.all_to_all(summed, ALL, 0, 0, tiled=True)

    new_cold_table, new_cold_accum = pl.pallas_call(
        functools.partial(cold_kernel, slot=slot, share=share),
        out_shape=(
            jax.ShapeDtypeStruct((shard, width), F32),
            jax.ShapeDtypeStruct((1, shard), F32),
        ),
        in_specs=[VMEM] * 4,
        out_specs=(VMEM, VMEM),
        compiler_params=params(),
        name="cold",
    )(asked, got, cold_table, cold_accum.reshape(1, shard))

    new_hot_table, new_hot_accum = pl.pallas_call(
        hot_kernel,
        out_shape=(
            jax.ShapeDtypeStruct((hot_rows, width), F32),
            jax.ShapeDtypeStruct((1, hot_rows), F32),
        ),
        in_specs=[VMEM] * 3,
        out_specs=(VMEM, VMEM),
        scratch_shapes=[pltpu.VMEM((hot_rows, width), F32)],
        compiler_params=params(),
        name="hot",
    )(hot_grad, hot_table, hot_accum.reshape(1, hot_rows))
    return (
        new_hot_table,
        new_hot_accum.reshape(hot_rows),
        new_cold_table,
        new_cold_accum.reshape(shard),
    )


def solution(mesh):
    return jax.shard_map(
        on_device,
        mesh=mesh,
        in_specs=(
            P(ALL, None),
            P(ALL, None),
            P(ALL, None),
            P(),
            P(),
            P("rows", None),
            P("rows"),
            P(),
            P(),
            P(),
            P(),
            P(ALL, None),
        ),
        out_specs=(P(), P(), P("rows", None), P("rows")),
        check_vma=False,
    )
```

time: 69.5 us -> 60.1 us (0.86)
  local copies, waits for them, and re-layouts: 9.49 us -> 1.28 us
  waiting for transfers between devices: 14.9 us -> 11.7 us
  Pallas kernels: 9.78 us -> 12 us
    unnamed x26 -> x8, local copies, waits for them, and re-layouts: 8.22 us -> 0.02 us
    pallas_call x0 -> x1, Pallas kernels: none -> 3.8 us  [on_device(): pl.pallas_call(functools.partial(early_kernel, n_owner=n_rows, slot=slot)...]
    all_to_all x1, waiting for transfers between devices: 7.02 us -> 3.37 us  [on_device(): lax.all_to_all(jnp.broadcast_to(fetch_rows.reshape(1, 1, asks), (n_dev, 1...]
    pallas_call x1, Pallas kernels: 1.15 us -> 0.3 us  [on_device(): pl.pallas_call(functools.partial(gather_kernel, n_rows=n_rows, n_rep=n_re...]
  transfers between devices with their start and end apart: 2 -> 2, of which waited for: 2 -> 2; matrix products, arithmetic and copies ran while one was open for 0% -> 0% of each run, Pallas kernels for 4% -> 10%
where the time goes in v2:
time: 60.1 us; the launch traced here: 59.8 us
  blocking collectives  24.2 us (40%)
  Pallas kernels  12 us (20%)
  waiting for transfers between devices  11.7 us (19%)
  starting transfers between devices  9.91 us (16%)
  local copies, waits for them, and re-layouts  1.28 us (2%)
  between operations  0.71 us (1%)
    all_to_all x1, blocking collectives, on_device(): got = lax.all_to_all(sent, ALL, 0, 0, tiled=True)  15.1 us
    all_to_all x1, blocking collectives, on_device(): fetched = lax.all_to_all(found, 'rows', 0, 0, tiled=True)  9.06 us
    all_to_all x1, waiting for transfers between devices, on_device(): hot_grad = lax.all_to_all(summed, ALL, 0, 0, tiled=True)  8.37 us
    all_to_all x1, starting transfers between devices, on_device(): lax.all_to_all(jnp.broadcast_to(fetch_rows.reshape(1, 1, asks), (n_dev, 1...  7.33 us
    pallas_call x1, Pallas kernels, on_device(): pl.pallas_call(functools.partial(layer_kernel, n_dev=n_dev, n_rep=n_rep,...  3.95 us
    pallas_call x1, Pallas kernels, on_device(): pl.pallas_call(functools.partial(early_kernel, n_owner=n_rows, slot=slot)...  3.8 us
    all_to_all x1, waiting for transfers between devices, on_device(): lax.all_to_all(jnp.broadcast_to(fetch_rows.reshape(1, 1, asks), (n_dev, 1...  3.37 us
    all_to_all x1, starting transfers between devices, on_device(): hot_grad = lax.all_to_all(summed, ALL, 0, 0, tiled=True)  2.59 us
  transfers between devices with their start and end apart: 2, of which 2 were waited for; matrix products, arithmetic and copies ran while one was open for 0% of the time, Pallas kernels for 10%

profile of v2, /device:TPU:0, one launch (start us, length us, event | category | flops | bytes accessed | tf_op | source)
XLA Modules:
  0.0 59.8 jit_solution(15206230027649674454)
XLA Ops:
  0.6 1.3 %broadcast_in_dim.8 = s32[32,1,16]{2,1,0:T(1,128)} broadcast(s32[16]{0:T(128)} %bitcast.9), dimensions={2} | broadcast | bytes 2112 | tf_op jit(solution)/shard_map/asks/broadcast_in_dim | solution.py:445
  1.9 7.3 %all-to-all-start = ((s32[32,1,16]{2,1,0:T(1,128)}), s32[32,1,16]{2,1,0:T(1,128)S(1)}, u32[]{:S(2)}, u32[]{:S(2)}) async-start(s32[32,1,16]{2,1,0:T(1,128)} %broadcast_in_dim.8), calls=%async_computation | async-start | bytes 32768 | tf_op jit(solution)/shard_map/asks/all_to_all | solution.py:444
  9.2 3.8 %early.1 = (bf16[512,2048]{1,0:T(8,128)(2,1)S(1)}, bf16[128,2048]{1,0:T(8,128)(2,1)S(1)}, bf16[128,16]{1,0:T(8,128)(2,1)S(1)}, f32[16,128]{1,0:T(8,128)S(1)}, f3...) custom-call(s32[1,128]{1,0:T(1,128)} %event_hbm.1, ...), custom_call_target="tpu_custom_call" | custom-call | flops 4000000000 | bytes 8388608 | tf_op jit(solution)/shard_map/early/pallas_call | solution.py:455
  13.0 3.4 %all-to-all-done.asked_ref = s32[32,1,16]{2,1,0:T(1,128)S(1)} async-done(((s32[32,1,16]{2,1,0:T(1,128)}), s32[32,1,16]{2,1,0:T(1,128)S(1)}, u32[]{:S(2)}, u32[]{:S(2)}) %all-to-all-start) | async-done | bytes 2080 | tf_op jit(solution)/shard_map/asks/all_to_all | solution.py:444
  16.4 0.3 gather.1
  16.7 9.1 %all_to_all.20.fetched_ref = f32[8,8,128]{2,1,0:T(8,128)S(1)} all-to-all(f32[8,8,128]{2,1,0:T(8,128)S(1)} %gather.1), channel_id=1, replica_groups=mesh['rows'=8,'rep'=4] {'rows'}, dimensions={0} | all-to-all | bytes 65536 | tf_op jit(solution)/shard_map/all_to_all | solution.py:512
  25.8 0.0 copy-start.2
  25.8 3.9 %layer.1 = f32[32,24,128]{2,1,0:T(8,128)S(1)} custom-call(f32[8,8,128]{2,1,0:T(8,128)S(1)} %all_to_all.20.fetched_ref, bf16[512,2048]{1,0:T(8,128)(2,1)S(1)} %get-tuple-element.22.w_in_ref, bf16[128,2048]{1,0:T(8,128)(2,1)S(1)} %get-tuple-element.23.proj_ref, bf16[128,16]{1,0:T(8,128)(2,1)S(1)} %get-tuple-element.24.pick_ref, ...), custom_call_target="tpu_custom_call" | custom-call | tf_op jit(solution)/shard_map/layer/pallas_call | solution.py:514
  29.7 0.0 copy-start
  29.7 0.0 copy-start.1
  29.8 0.0 copy-start.3
  29.8 15.1 %all_to_all.21.got_ref = f32[32,24,128]{2,1,0:T(8,128)S(1)} all-to-all(f32[32,24,128]{2,1,0:T(8,128)S(1)} %layer.1), channel_id=1, replica_groups=mesh['rows'=8,'rep'=4] {'rows','rep'}, dimensions={0} | all-to-all | bytes 786432 | tf_op jit(solution)/shard_map/all_to_all | solution.py:525
  44.9 0.8 %sum.1 = f32[32,16,128]{2,1,0:T(8,128)} custom-call(f32[32,24,128]{2,1,0:T(8,128)S(1)} %all_to_all.21.got_ref), custom_call_target="tpu_custom_call" | custom-call | tf_op jit(solution)/shard_map/sum/pallas_call | solution.py:527
  45.6 2.6 %all-to-all-start.3 = ((f32[32,16,128]{2,1,0:T(8,128)}), f32[32,16,128]{2,1,0:T(8,128)S(1)}, u32[]{:S(2)}, u32[]{:S(2)}) async-start(f32[32,16,128]{2,1,0:T(8,128)} %sum.1), calls=%async_computation.3 | async-start | bytes 524288 | tf_op jit(solution)/shard_map/all_to_all | solution.py:535
  48.2 0.0 copy-done.2
  48.2 0.0 copy-done
  48.2 2.2 %cold.1 = (f32[256,512]{1,0:T(8,128)}, f32[1,256]{1,0:T(1,128)}) custom-call(s32[32,1,16]{2,1,0:T(1,128)S(1)} %all-to-all-done.asked_ref, f32[32,24,128]{2,1,0:T(8,128)S(1)} %all_to_all.21.got_ref, f32[256,512]{1,0:T(8,128)S(1)} %copy-done, f32[1,256]{1,0:T(1,128)S(1)} %bitcast.7), custom_call_target="tpu_custom_call" | custom-call | tf_op jit(solution)/shard_map/cold/pallas_call | solution.py:537
  50.4 8.4 %all-to-all-done.3.got_ref = f32[32,16,128]{2,1,0:T(8,128)S(1)} async-done(((f32[32,16,128]{2,1,0:T(8,128)}), f32[32,16,128]{2,1,0:T(8,128)S(1)}, u32[]{:S(2)}, u32[]{:S(2)}) %all-to-all-start.3) | async-done | bytes 262176 | tf_op jit(solution)/shard_map/all_to_all | solution.py:535
  58.8 0.0 copy-done.1
  58.8 0.0 copy-done.3
  58.8 1.0 %hot.1 = (f32[128,512]{1,0:T(8,128)}, f32[1,128]{1,0:T(1,128)}) custom-call(f32[32,16,128]{2,1,0:T(8,128)S(1)} %all-to-all-done.3.got_ref, f32[128,512]{1,0:T(8,128)S(1)} %copy-done.1, f32[1,128]{1,0:T(1,128)S(1)} %bitcast.8), custom_call_target="tpu_custom_call" | custom-call | tf_op jit(solution)/shard_map/hot/pallas_call | solution.py:549
Async XLA Ops:
  1.9 14.5 %all-to-all-start = ((s32[32,1,16]{2,1,0:T(1,128)}), s32[32,1,16]{2,1,0:T(1,128)S(1)}, u32[]{:S(2)}, u32[]{:S(2)}) async-start(s32[32,1,16]{2,1,0:T(1,128)} %broadcast_in_dim.8), calls=%async_computation | async-start | bytes 32768 | tf_op jit(solution)/shard_map/asks/all_to_all | solution.py:444
  25.8 22.4 %copy-start.2 = (f32[256]{0:T(256)S(1)}, f32[256]{0:T(256)}, u32[]{:S(2)}) copy-start(f32[256]{0:T(256)} %param.18) | copy-start | bytes 3076
  29.7 18.5 %copy-start = (f32[256,512]{1,0:T(8,128)S(1)}, f32[256,512]{1,0:T(8,128)}, u32[]{:S(2)}) copy-start(f32[256,512]{1,0:T(8,128)} %table_ref.3) | copy-start | bytes 1572868
  29.7 29.0 %copy-start.1 = (f32[128,512]{1,0:T(8,128)S(1)}, f32[128,512]{1,0:T(8,128)}, u32[]{:S(2)}) copy-start(f32[128,512]{1,0:T(8,128)} %table_ref.2) | copy-start | bytes 786436
  29.8 29.0 %copy-start.3 = (f32[128]{0:T(128)S(1)}, f32[128]{0:T(128)}, u32[]{:S(2)}) copy-start(f32[128]{0:T(128)} %param.16) | copy-start | bytes 1540
  45.6 13.2 %all-to-all-start.3 = ((f32[32,16,128]{2,1,0:T(8,128)}), f32[32,16,128]{2,1,0:T(8,128)S(1)}, u32[]{:S(2)}, u32[]{:S(2)}) async-start(f32[32,16,128]{2,1,0:T(8,128)} %sum.1), calls=%async_computation.3 | async-start | bytes 524288 | tf_op jit(solution)/shard_map/all_to_all | solution.py:535

commit v3 on v2

--- a/solution.py
+++ b/solution.py
@@ -32,6 +32,17 @@
 NN = ((1,), (0,))
 NT = ((1,), (1,))
 TN = ((0,), (0,))
+
+
+def ask_kernel(rows_hbm, out_ref, rows_scr, sem):
+    copy = pltpu.make_async_copy(rows_hbm, rows_scr, sem)
+    copy.start()
+    copy.wait()
+    out_ref[...] = jnp.broadcast_to(rows_scr[...][None], out_ref.shape)
+
+
+def even(n):
+    return n + n % 2
 
 
 def gather_kernel(asked_ref, table_ref, out_ref, rows_scr, *, n_rows, n_rep, slot):
@@ -319,62 +330,76 @@
     cold = back(d_hat[hot_rows:slots], cold_hat, cold_rstd) + base_ref[hot_rows:slots, :]
     x_scr[...] = cold * live
 
-    units = hot_rows * chunks
-    share = units // n_dev
-    if share < SUBLANES:
+    share = hot_rows * chunks // n_dev
+    if share % SUBLANES:
         g_scr[...] = hot
     for g in range(hot_rows // SUBLANES):
         for c in range(chunks):
             first = (g * chunks + c) * SUBLANES
             at = (slice(g * SUBLANES, (g + 1) * SUBLANES), slice(c * LANES, (c + 1) * LANES))
-            if share >= SUBLANES:
-                out_ref[first // share, first % share : first % share + SUBLANES, :] = hot[at]
+            if share % SUBLANES == 0:
+                off = first % share // 2
+                out_ref[first // share, off : off + SUBLANES // 2] = hot[at].reshape(
+                    SUBLANES // 2, 2, LANES
+                )
             else:
                 for i in range(SUBLANES):
-                    q = first + i
+                    to, off = divmod(first + i, share)
                     row = g * SUBLANES + i
-                    out_ref[q // share, q % share : q % share + 1, :] = g_scr[row : row + 1, at[1]]
-
+                    out_ref[to, off // 2, off % 2 : off % 2 + 1, :] = g_scr[row : row + 1, at[1]]
+
+    part = chunks // n_rep
+    base = even(share) // 2
     for j in range(n_owner):
-        for k in range(slot):
-            for c in range(chunks):
-                at = j * slot + k
-                row = x_scr[at : at + 1, c * LANES : (c + 1) * LANES]
-                to = share + k * chunks + c
-                for p in range(n_rep):
-                    out_ref[j * n_rep + p, to : to + 1, :] = row
-
-
-def sum_kernel(got_ref, out_ref, *, share):
-    n_dev = out_ref.shape[0]
-    total = got_ref[0, 0:share, :]
+        for c in range(chunks):
+            to = j * n_rep + c // part
+            cols = slice(c * LANES, (c + 1) * LANES)
+            if part == 1 and slot == 2:
+                out_ref[to, base] = x_scr[j * slot : (j + 1) * slot, cols]
+            else:
+                for k in range(slot):
+                    off = k * part + c % part
+                    at = j * slot + k
+                    out_ref[to, base + off // 2, off % 2 : off % 2 + 1, :] = x_scr[at : at + 1, cols]
+
+
+def sum_kernel(got_ref, out_ref, cold_ref):
+    n_dev, share, _ = out_ref.shape
+    base = even(share) // 2
+    total = got_ref[0, 0:base]
     for d in range(1, n_dev):
-        total = total + got_ref[d, 0:share, :]
+        total = total + got_ref[d, 0:base]
+    total = total.reshape(2 * base, LANES)[0:share]
     for d in range(n_dev):
         out_ref[d] = total
-
-
-def cold_kernel(asked_ref, got_ref, table_ref, accum_ref, new_ref, new_accum_ref, *, slot, share):
+    cold_ref[...] = got_ref[:, base:]
+
+
+def cold_kernel(asked_ref, *refs, slot, n_rep):
+    part_refs = refs[:n_rep]
+    table_ref, accum_ref, new_ref, new_accum_ref, part_scr = refs[n_rep:]
     j = lax.axis_index("rows")
+    p = lax.axis_index("rep")
     n_dev = asked_ref.shape[0]
     shard, width = table_ref.shape
     chunks = width // LANES
+    part = chunks // n_rep
+    for s in range(n_rep):
+        part_scr[(p + n_rep - s) % n_rep] = part_refs[s][...]
     asked = asked_ref[:, 0, :]
     pos = lax.broadcasted_iota(jnp.int32, asked.shape, 1)
     picks = []
     for k in range(slot):
         col = jnp.sum(jnp.where(pos == j * slot + k, asked, 0), axis=1, keepdims=True)
-        picks.append(
-            (lax.broadcasted_iota(jnp.int32, (n_dev, shard), 1) == col).astype(F32)
-        )
+        picks.append((lax.broadcasted_iota(jnp.int32, (n_dev, shard), 1) == col).astype(F32))
+    pick = jnp.concatenate(picks, axis=0)
     grads = []
     for c in range(chunks):
-        part = None
+        rows = []
         for k in range(slot):
-            rows = got_ref[:, share + k * chunks + c, :]
-            one = dot(picks[k], rows, TN, lax.Precision.HIGHEST)
-            part = one if part is None else part + one
-        grads.append(part)
+            off = k * part + c % part
+            rows.append(part_scr[c // part, :, off // 2, off % 2, :])
+        grads.append(dot(pick, jnp.concatenate(rows, axis=0), TN, lax.Precision.HIGHEST))
     total = grads[0] * grads[0]
     for g in grads[1:]:
         total = total + g * g
@@ -436,14 +461,22 @@
     shard = cold_table.shape[0]
     chunks = width // LANES
     share = hot_rows * chunks // n_dev
+    cold_pairs = even(slot * (chunks // n_rep)) // 2
     asks = fetch_rows.shape[1]
     slots = hot_rows + asks
     seq, inner = out_grad.shape[0], w_out.shape[0]
 
     with jax.named_scope("asks"):
-        asked = lax.all_to_all(
-            jnp.broadcast_to(fetch_rows.reshape(1, 1, asks), (n_dev, 1, asks)), ALL, 0, 0, tiled=True
-        )
+        mine = pl.pallas_call(
+            ask_kernel,
+            out_shape=pltpu.VMEM((n_dev, 1, asks), jnp.int32),
+            in_specs=[ANY],
+            out_specs=VMEM,
+            scratch_shapes=[pltpu.VMEM((1, asks), jnp.int32), pltpu.SemaphoreType.DMA],
+            compiler_params=params(),
+            name="ask",
+        )(pltpu.with_memory_space_constraint(fetch_rows, pltpu.HBM))
+        asked = lax.all_to_all(mine, ALL, 0, 0, tiled=True)
     late = (
         ((seq, inner), BF16),
         ((slots, seq), BF16),
@@ -513,7 +546,7 @@
 
     sent = pl.pallas_call(
         functools.partial(layer_kernel, n_dev=n_dev, n_rep=n_rep, slot=slot),
-        out_shape=jax.ShapeDtypeStruct((n_dev, share + slot * chunks, LANES), F32),
+        out_shape=jax.ShapeDtypeStruct((n_dev, even(share) // 2 + cold_pairs, 2, LANES), F32),
         in_specs=[VMEM] * 7 + [ANY] * 6,
         out_specs=VMEM,
         scratch_shapes=[pltpu.VMEM((asks, width), F32), pltpu.VMEM((hot_rows, width), F32)]
@@ -524,27 +557,35 @@
     )(fetched, *early[:6], *early[7:])
     got = lax.all_to_all(sent, ALL, 0, 0, tiled=True)
 
-    summed = pl.pallas_call(
-        functools.partial(sum_kernel, share=share),
-        out_shape=jax.ShapeDtypeStruct((n_dev, share, LANES), F32),
+    summed, cold_part = pl.pallas_call(
+        sum_kernel,
+        out_shape=(
+            pltpu.VMEM((n_dev, share, LANES), F32),
+            pltpu.VMEM((n_dev, cold_pairs, 2, LANES), F32),
+        ),
         in_specs=[VMEM],
-        out_specs=VMEM,
+        out_specs=(VMEM, VMEM),
         compiler_params=params(),
         name="sum",
     )(got)
     hot_grad = lax.all_to_all(summed, ALL, 0, 0, tiled=True)
+    parts = [cold_part] + [
+        lax.ppermute(cold_part, "rep", [(i, (i + s) % n_rep) for i in range(n_rep)])
+        for s in range(1, n_rep)
+    ]
 
     new_cold_table, new_cold_accum = pl.pallas_call(
-        functools.partial(cold_kernel, slot=slot, share=share),
+        functools.partial(cold_kernel, slot=slot, n_rep=n_rep),
         out_shape=(
             jax.ShapeDtypeStruct((shard, width), F32),
             jax.ShapeDtypeStruct((1, shard), F32),
         ),
-        in_specs=[VMEM] * 4,
+        in_specs=[VMEM] * (n_rep + 3),
         out_specs=(VMEM, VMEM),
+        scratch_shapes=[pltpu.VMEM((n_rep, n_dev, cold_pairs, 2, LANES), F32)],
         compiler_params=params(),
         name="cold",
-    )(asked, got, cold_table, cold_accum.reshape(1, shard))
+    )(asked, *parts, cold_table, cold_accum.reshape(1, shard))
 
     new_hot_table, new_hot_accum = pl.pallas_call(
         hot_kernel,

time: 60.1 us -> 58.3 us (0.970)
  blocking collectives: 24.2 us -> 22.3 us
  starting transfers between devices: 9.91 us -> 11.8 us
  waiting for transfers between devices: 11.7 us -> 10.3 us
  local copies, waits for them, and re-layouts: 1.28 us -> 0.02 us
  Pallas kernels: 12 us -> 12.8 us
    all_to_all x1, waiting for transfers between devices: 8.37 us -> 2.82 us  [on_device(): hot_grad = lax.all_to_all(summed, ALL, 0, 0, tiled=True)]
    ppermute x0 -> x3, waiting for transfers between devices: none -> 4.08 us  [on_device(): lax.ppermute(cold_part, 'rep', [(i, (i + s) % n_rep) for i in range(n_rep)])]
    ppermute x0 -> x3, starting transfers between devices: none -> 1.92 us  [on_device(): lax.ppermute(cold_part, 'rep', [(i, (i + s) % n_rep) for i in range(n_rep)])]
    all_to_all x1, blocking collectives: 15.1 us -> 13.2 us  [on_device(): got = lax.all_to_all(sent, ALL, 0, 0, tiled=True)]
    broadcast_in_dim x1 -> x0, local copies, waits for them, and re-layouts: 1.26 us -> none  [on_device(): jnp.broadcast_to(fetch_rows.reshape(1, 1, asks), (n_dev, 1, asks))]
    pallas_call x2 -> x3, Pallas kernels: 2.93 us -> 3.79 us  [the longest x1 1.74 us: on_device(): pl.pallas_call(functools.partial(cold_kernel, slot=slot, n_rep=n_rep), ou...]
  transfers between devices with their start and end apart: 2 -> 5, of which waited for: 2 -> 4; matrix products, arithmetic and copies ran while one was open for 0% -> 0% of each run, Pallas kernels for 10% -> 10%
where the time goes in v3:
time: 58.3 us; the launch traced here: 57.9 us
  blocking collectives  22.3 us (38%)
  Pallas kernels  12.8 us (22%)
  starting transfers between devices  11.8 us (20%)
  waiting for transfers between devices  10.3 us (18%)
  between operations  0.7 us (1%)
    all_to_all x1, blocking collectives, on_device(): got = lax.all_to_all(sent, ALL, 0, 0, tiled=True)  13.2 us
    all_to_all x1, blocking collectives, on_device(): fetched = lax.all_to_all(found, 'rows', 0, 0, tiled=True)  9.06 us
    all_to_all x1, starting transfers between devices, on_device(): asked = lax.all_to_all(mine, ALL, 0, 0, tiled=True)  7.33 us
    ppermute x3, waiting for transfers between devices, on_device(): lax.ppermute(cold_part, 'rep', [(i, (i + s) % n_rep) for i in range(n_rep)])  4.08 us
    pallas_call x1, Pallas kernels, on_device(): pl.pallas_call(functools.partial(layer_kernel, n_dev=n_dev, n_rep=n_rep,...  3.93 us
    pallas_call x1, Pallas kernels, on_device(): pl.pallas_call(functools.partial(early_kernel, n_owner=n_rows, slot=slot)...  3.8 us
    all_to_all x1, waiting for transfers between devices, on_device(): asked = lax.all_to_all(mine, ALL, 0, 0, tiled=True)  3.36 us
    all_to_all x1, waiting for transfers between devices, on_device(): hot_grad = lax.all_to_all(summed, ALL, 0, 0, tiled=True)  2.82 us
  transfers between devices with their start and end apart: 5, of which 4 were waited for; matrix products, arithmetic and copies ran while one was open for 0% of the time, Pallas kernels for 10%

profile of v3, /device:TPU:0, one launch (start us, length us, event | category | flops | bytes accessed | tf_op | source)
XLA Modules:
  0.0 57.9 jit_solution(11618416456795494242)
XLA Ops:
  0.6 1.3 %ask.1 = s32[32,1,16]{2,1,0:T(1,128)} custom-call(s32[1,16]{1,0:T(1,128)} %rows_hbm.1), custom_call_target="tpu_custom_call" | custom-call | tf_op jit(solution)/shard_map/asks/ask/pallas_call | solution.py:470
  1.9 7.3 %all-to-all-start = ((s32[32,1,16]{2,1,0:T(1,128)}), s32[32,1,16]{2,1,0:T(1,128)S(1)}, u32[]{:S(2)}, u32[]{:S(2)}) async-start(s32[32,1,16]{2,1,0:T(1,128)} %ask.1), calls=%async_computation | async-start | bytes 32768 | tf_op jit(solution)/shard_map/asks/all_to_all | solution.py:479
  9.3 3.8 %early.1 = (bf16[512,2048]{1,0:T(8,128)(2,1)S(1)}, bf16[128,2048]{1,0:T(8,128)(2,1)S(1)}, bf16[128,16]{1,0:T(8,128)(2,1)S(1)}, f32[16,128]{1,0:T(8,128)S(1)}, f3...) custom-call(s32[1,128]{1,0:T(1,128)} %event_hbm.1, ...), custom_call_target="tpu_custom_call" | custom-call | flops 4000000000 | bytes 8388608 | tf_op jit(solution)/shard_map/early/pallas_call | solution.py:488
  13.1 3.4 %all-to-all-done.asked_ref = s32[32,1,16]{2,1,0:T(1,128)S(1)} async-done(((s32[32,1,16]{2,1,0:T(1,128)}), s32[32,1,16]{2,1,0:T(1,128)S(1)}, u32[]{:S(2)}, u32[]{:S(2)}) %all-to-all-start) | async-done | bytes 2080 | tf_op jit(solution)/shard_map/asks/all_to_all | solution.py:479
  16.4 0.3 gather.1
  16.7 9.1 %all_to_all.20.fetched_ref = f32[8,8,128]{2,1,0:T(8,128)S(1)} all-to-all(f32[8,8,128]{2,1,0:T(8,128)S(1)} %gather.1), channel_id=1, replica_groups=mesh['rows'=8,'rep'=4] {'rows'}, dimensions={0} | all-to-all | bytes 65536 | tf_op jit(solution)/shard_map/all_to_all | solution.py:545
  25.8 3.9 %layer.1 = f32[32,9,2,128]{3,2,1,0:T(2,128)S(1)} custom-call(f32[8,8,128]{2,1,0:T(8,128)S(1)} %all_to_all.20.fetched_ref, bf16[512,2048]{1,0:T(8,128)(2,1)S(1)} %get-tuple-element.24.w_in_ref, bf16[128,2048]{1,0:T(8,128)(2,1)S(1)} %get-tuple-element.25.proj_ref, bf16[128,16]{1,0:T(8,128)(2,1)S(1)} %get-tuple-element.26.pick_ref, ...), custom_call_target="tpu_custom_call" | custom-call | tf_op jit(solution)/shard_map/layer/pallas_call | solution.py:547
  29.7 0.0 copy-start.1
  29.8 13.2 %all_to_all.21.got_ref = f32[32,9,2,128]{3,2,1,0:T(2,128)S(1)} all-to-all(f32[32,9,2,128]{3,2,1,0:T(2,128)S(1)} %layer.1), channel_id=1, replica_groups=mesh['rows'=8,'rep'=4] {'rows','rep'}, dimensions={0} | all-to-all | bytes 589824 | tf_op jit(solution)/shard_map/all_to_all | solution.py:558
  43.0 0.8 %sum.1 = (f32[32,16,128]{2,1,0:T(8,128)}, f32[32,1,2,128]{3,2,1,0:T(2,128)S(1)}) custom-call(f32[32,9,2,128]{3,2,1,0:T(2,128)S(1)} %all_to_all.21.got_ref), custom_call_target="tpu_custom_call" | custom-call | tf_op jit(solution)/shard_map/sum/pallas_call | solution.py:560
  43.8 2.6 %all-to-all-start.3 = ((f32[32,16,128]{2,1,0:T(8,128)}), f32[32,16,128]{2,1,0:T(8,128)S(1)}, u32[]{:S(2)}, u32[]{:S(2)}) async-start(f32[32,16,128]{2,1,0:T(8,128)} %get-tuple-element.36), calls=%async_computation.3 | async-start | bytes 524288 | tf_op jit(solution)/shard_map/all_to_all | solution.py:571
  46.4 1.4 %collective-permute-start.2 = (f32[32,1,2,128]{3,2,1,0:T(2,128)S(1)}, f32[32,1,2,128]{3,2,1,0:T(2,128)S(1)}, u32[]{:S(2)}, u32[]{:S(2)}) collective-permute-start(f32[32,1,2,128]{3,2,1,0:T(2,128)S(1)} %get-tuple-element.39.refs_0_), channel_id=1, source_target_pairs={{0,3},{1,0},{2,1},{3,2},{4,7},{5,4},{6,5},{7,6},{8,11},{9,8},{10,9... | collective-permute-start | bytes 98312 | tf_op jit(solution)/shard_map/ppermute | solution.py:573
  47.8 0.4 collective-permute-start.1
  48.2 0.1 collective-permute-start
  48.3 1.7 %collective-permute-done.2.refs_3_ = f32[32,1,2,128]{3,2,1,0:T(2,128)S(1)} collective-permute-done((f32[32,1,2,128]{3,2,1,0:T(2,128)S(1)}, f32[32,1,2,128]{3,2,1,0:T(2,128)S(1)}, u32[]{:S(2)}, u32[]{:S(2)}) %collective-permute-start.2) | collective-permute-done | bytes 32800 | tf_op jit(solution)/shard_map/ppermute | solution.py:573
  50.0 2.3 %collective-permute-done.1.refs_2_ = f32[32,1,2,128]{3,2,1,0:T(2,128)S(1)} collective-permute-done((f32[32,1,2,128]{3,2,1,0:T(2,128)S(1)}, f32[32,1,2,128]{3,2,1,0:T(2,128)S(1)}, u32[]{:S(2)}, u32[]{:S(2)}) %collective-permute-start.1) | collective-permute-done | bytes 32800 | tf_op jit(solution)/shard_map/ppermute | solution.py:573
  52.4 0.0 collective-permute-done.refs_1_
  52.4 0.0 copy-done
  52.4 0.0 copy-done.2
  52.4 1.7 %cold.1 = (f32[256,512]{1,0:T(8,128)}, f32[1,256]{1,0:T(1,128)}) custom-call(s32[32,1,16]{2,1,0:T(1,128)S(1)} %all-to-all-done.asked_ref, f32[32,1,2,128]{3,2,1,0:T(2,128)S(1)} %get-tuple-element.39.refs_0_, f32[32,1,2,128]{3,2,1,0:T(2,128)S(1)} %collective-permute-done.refs_1_, f32[32,1,2,128]{3,2,1,0:T(2,128)S(1)} %collective-permute-done.1.refs_2_, ...), custom_call_target="tpu_custom_call" | custom-call | tf_op jit(solution)/shard_map/cold/pallas_call | solution.py:577
  54.1 2.8 %all-to-all-done.3.got_ref = f32[32,16,128]{2,1,0:T(8,128)S(1)} async-done(((f32[32,16,128]{2,1,0:T(8,128)}), f32[32,16,128]{2,1,0:T(8,128)S(1)}, u32[]{:S(2)}, u32[]{:S(2)}) %all-to-all-start.3) | async-done | bytes 262176 | tf_op jit(solution)/shard_map/all_to_all | solution.py:571
  56.9 0.0 copy-done.3
  56.9 0.0 copy-done.1
  56.9 1.0 %hot.1 = (f32[128,512]{1,0:T(8,128)}, f32[1,128]{1,0:T(1,128)}) custom-call(f32[32,16,128]{2,1,0:T(8,128)S(1)} %all-to-all-done.3.got_ref, f32[128,512]{1,0:T(8,128)S(1)} %copy-done.1, f32[1,128]{1,0:T(1,128)S(1)} %bitcast.7), custom_call_target="tpu_custom_call" | custom-call | tf_op jit(solution)/shard_map/hot/pallas_call | solution.py:590
  (3 shorter events, 0.0 us)
Async XLA Ops:
  1.9 14.5 %all-to-all-start = ((s32[32,1,16]{2,1,0:T(1,128)}), s32[32,1,16]{2,1,0:T(1,128)S(1)}, u32[]{:S(2)}, u32[]{:S(2)}) async-start(s32[32,1,16]{2,1,0:T(1,128)} %ask.1), calls=%async_computation | async-start | bytes 32768 | tf_op jit(solution)/shard_map/asks/all_to_all | solution.py:479
  25.8 26.6 %copy-start = (f32[256,512]{1,0:T(8,128)S(1)}, f32[256,512]{1,0:T(8,128)}, u32[]{:S(2)}) copy-start(f32[256,512]{1,0:T(8,128)} %refs_4_.1) | copy-start | bytes 1572868
  25.8 26.6 %copy-start.2 = (f32[256]{0:T(256)S(1)}, f32[256]{0:T(256)}, u32[]{:S(2)}) copy-start(f32[256]{0:T(256)} %param.18) | copy-start | bytes 3076
  25.8 31.1 %copy-start.3 = (f32[128]{0:T(128)S(1)}, f32[128]{0:T(128)}, u32[]{:S(2)}) copy-start(f32[128]{0:T(128)} %param.16) | copy-start | bytes 1540
  29.7 27.2 %copy-start.1 = (f32[128,512]{1,0:T(8,128)S(1)}, f32[128,512]{1,0:T(8,128)}, u32[]{:S(2)}) copy-start(f32[128,512]{1,0:T(8,128)} %table_ref.1) | copy-start | bytes 786436
  43.8 13.2 %all-to-all-start.3 = ((f32[32,16,128]{2,1,0:T(8,128)}), f32[32,16,128]{2,1,0:T(8,128)S(1)}, u32[]{:S(2)}, u32[]{:S(2)}) async-start(f32[32,16,128]{2,1,0:T(8,128)} %get-tuple-element.36), calls=%async_computation.3 | async-start | bytes 524288 | tf_op jit(solution)/shard_map/all_to_all | solution.py:571
  46.4 3.7 %collective-permute-start.2 = (f32[32,1,2,128]{3,2,1,0:T(2,128)S(1)}, f32[32,1,2,128]{3,2,1,0:T(2,128)S(1)}, u32[]{:S(2)}, u32[]{:S(2)}) collective-permute-start(f32[32,1,2,128]{3,2,1,0:T(2,128)S(1)} %get-tuple-element.39.refs_0_), channel_id=1, source_target_pairs={{0,3},{1,0},{2,1},{3,2},{4,7},{5,4},{6,5},{7,6},{8,11},{9,8},{10,9... | collective-permute-start | bytes 98312 | tf_op jit(solution)/shard_map/ppermute | solution.py:573
  47.8 4.6 %collective-permute-start.1 = (f32[32,1,2,128]{3,2,1,0:T(2,128)S(1)}, f32[32,1,2,128]{3,2,1,0:T(2,128)S(1)}, u32[]{:S(2)}, u32[]{:S(2)}) collective-permute-start(f32[32,1,2,128]{3,2,1,0:T(2,128)S(1)} %get-tuple-element.39.refs_0_), channel_id=1, source_target_pairs={{0,2},{1,3},{2,0},{3,1},{4,6},{5,7},{6,4},{7,5},{8,10},{9,11},{10,... | collective-permute-start | bytes 98312 | tf_op jit(solution)/shard_map/ppermute | solution.py:573
  48.2 4.2 %collective-permute-start = (f32[32,1,2,128]{3,2,1,0:T(2,128)S(1)}, f32[32,1,2,128]{3,2,1,0:T(2,128)S(1)}, u32[]{:S(2)}, u32[]{:S(2)}) collective-permute-start(f32[32,1,2,128]{3,2,1,0:T(2,128)S(1)} %get-tuple-element.39.refs_0_), channel_id=1, source_target_pairs={{0,1},{1,2},{2,3},{3,0},{4,5},{5,6},{6,7},{7,4},{8,9},{9,10},{10,1... | collective-permute-start | bytes 98312 | tf_op jit(solution)/shard_map/ppermute | solution.py:573

commit v4 on v1

v4 whole, which is shorter than its diff:
```python
import functools

import jax
import jax.numpy as jnp
from jax import lax
from jax.experimental import pallas as pl
from jax.experimental.pallas import tpu as pltpu
from jax.sharding import PartitionSpec as P

HEAD = 128
STEP_RATE = 0.5
LANES = 128
SUBLANES = 8
ALL = ("rows", "rep")
F32 = jnp.float32
BF16 = jnp.bfloat16

LONG = pl.CostEstimate(flops=10**10, bytes_accessed=16 << 20, transcendentals=0)

VMEM = pl.BlockSpec(memory_space=pltpu.VMEM)
ANY = pl.BlockSpec(memory_space=pl.ANY)


def params(mib=24):
    return pltpu.CompilerParams(vmem_limit_bytes=mib << 20)


def dot(a, b, dims, precision=None):
    return lax.dot_general(
        a, b, (dims, ((), ())), preferred_element_type=F32, precision=precision
    )


NN = ((1,), (0,))
NT = ((1,), (1,))
TN = ((0,), (0,))


def ask_kernel(rows_hbm, out_ref, rows_scr, sem):
    copy = pltpu.make_async_copy(rows_hbm, rows_scr, sem)
    copy.start()
    copy.wait()
    out_ref[...] = jnp.broadcast_to(rows_scr[...][None], out_ref.shape)


def even(n):
    return n + n % 2


def gather_kernel(asked_ref, table_ref, out_ref, rows_scr, *, n_rows, n_rep, slot):
    j = lax.axis_index("rows")
    p = lax.axis_index("rep")
    shard = table_ref.shape[0]
    width = table_ref.shape[1]
    chunks = width // LANES

    for r in range(n_rows):
        rows_scr[r : r + 1, :] = asked_ref[r * n_rep + p]
    asked = rows_scr[...]
    pos = lax.broadcasted_iota(jnp.int32, asked.shape, 1)
    picks = []
    for k in range(slot):
        col = jnp.sum(jnp.where(pos == j * slot + k, asked, 0), axis=1, keepdims=True)
        picks.append((lax.broadcasted_iota(jnp.int32, (n_rows, shard), 1) == col).astype(F32))
    pick = jnp.concatenate(picks, axis=0).astype(BF16)
    table = table_ref[...]
    high = table.astype(BF16)
    rest = table - high.astype(F32)
    mid = rest.astype(BF16)
    low = (rest - mid.astype(F32)).astype(BF16)
    rows = dot(pick, high, NN) + dot(pick, mid, NN) + dot(pick, low, NN)
    for k in range(slot):
        for c in range(chunks):
            out_ref[:, k * chunks + c, :] = rows[
                k * n_rows : (k + 1) * n_rows, c * LANES : (c + 1) * LANES
            ]


def normalise(x, eps):
    cent = x - jnp.mean(x, axis=1, keepdims=True)
    rstd = lax.rsqrt(jnp.mean(cent * cent, axis=1, keepdims=True) + eps)
    return cent * rstd, rstd


def project(x_hat, gain, bias, w_in):
    pre = dot((x_hat * gain + bias).astype(BF16), w_in, NN)
    sig = jax.nn.sigmoid(pre)
    return (pre * sig).astype(BF16), sig * (1.0 + pre * (1.0 - sig))


def layer_kernel(
    event_ref,
    count_ref,
    hot_ref,
    fetched_ref,
    gain_ref,
    bias_ref,
    w_in_ref,
    w_out_ref,
    grad_ref,
    out_ref,
    x_scr,
    g_scr,
    c_scr,
    *,
    n_dev,
    n_rep,
    slot,
):
    hot_rows, width = hot_ref.shape
    n_owner = fetched_ref.shape[0]
    chunks = width // LANES
    slots = x_scr.shape[0]
    fetched = slots - hot_rows
    seq = grad_ref.shape[0]
    inner = w_out_ref.shape[0]
    heads = inner // HEAD
    gain = gain_ref[...]

    owner = lax.broadcasted_iota(jnp.int32, (fetched, n_owner), 0) // slot
    mine = owner == lax.broadcasted_iota(jnp.int32, (fetched, n_owner), 1)
    counts = jnp.broadcast_to(count_ref[...], (fetched, n_owner))
    count_col = jnp.sum(jnp.where(mine, counts, 0), axis=1, keepdims=True)
    live = (lax.broadcasted_iota(jnp.int32, (fetched, 1), 0) % slot < count_col).astype(F32)

    for j in range(n_owner):
        for k in range(slot):
            at = j * slot + k
            for c in range(chunks):
                c_scr[at : at + 1, c * LANES : (c + 1) * LANES] = fetched_ref[
                    j, k * chunks + c : k * chunks + c + 1, :
                ]
    x_scr[0:hot_rows, :] = hot_ref[...]
    x_scr[hot_rows:slots, :] = c_scr[...] * live
    x_hat, rstd = normalise(x_scr[...], 1e-05)
    proj, dsilu = project(x_hat, gain, bias_ref[...], w_in_ref[...])

    scatter = (
        lax.broadcasted_iota(jnp.int32, (slots, seq), 0)
        == jnp.broadcast_to(event_ref[...], (slots, seq))
    ).astype(F32)
    scatter_b = scatter.astype(BF16)
    proj_ev = dot(scatter_b, proj, TN).astype(BF16)
    gates = proj_ev[:, 0:inner].astype(F32)

    scale = HEAD ** (-0.5)
    causal = (
        lax.broadcasted_iota(jnp.int32, (seq, seq), 0)
        >= lax.broadcasted_iota(jnp.int32, (seq, seq), 1)
    ).astype(F32) * (1.0 / seq)

    values, queries, keys, atts, dacts, mixeds = [], [], [], [], [], []
    for h in range(heads):
        lo = h * HEAD
        v = proj_ev[:, inner + lo : inner + lo + HEAD]
        q = proj_ev[:, 2 * inner + lo : 2 * inner + lo + HEAD]
        kk = proj_ev[:, 3 * inner + lo : 3 * inner + lo + HEAD]
        s = dot(q, kk, NT) * scale
        sg = jax.nn.sigmoid(s)
        a = (s * sg * causal).astype(BF16)
        dacts.append(sg * (1.0 + s * (1.0 - sg)) * causal)
        values.append(v)
        queries.append(q)
        keys.append(kk)
        atts.append(a)
        mixeds.append(dot(a, v, NN))
    y, mrstd = normalise(jnp.concatenate(mixeds, axis=1), 1e-06)

    grad = grad_ref[...]
    d_gated = dot(grad, w_out_ref[...], NT).astype(BF16).astype(F32)
    d_gates = (d_gated * y).astype(BF16)
    d_y = d_gated * gates
    d_mixed = mrstd * (
        d_y - jnp.mean(d_y, axis=1, keepdims=True) - y * jnp.mean(d_y * y, axis=1, keepdims=True)
    )
    d_mixed = d_mixed.astype(BF16)
    d_vs, d_qs, d_ks = [], [], []
    for h in range(heads):
        dm = d_mixed[:, h * HEAD : (h + 1) * HEAD]
        d_a = dot(dm, values[h], NT).astype(BF16).astype(F32)
        d_vs.append(dot(atts[h], dm, TN).astype(BF16))
        d_s = (d_a * dacts[h] * scale).astype(BF16)
        d_qs.append(dot(d_s, keys[h], NN).astype(BF16))
        d_ks.append(dot(d_s, queries[h], TN).astype(BF16))
    d_proj = jnp.concatenate([d_gates] + d_vs + d_qs + d_ks, axis=1)

    d_slot = dot(scatter_b, d_proj, NN)
    d_hat = dot((d_slot * dsilu).astype(BF16), w_in_ref[...], NT) * gain
    d_x = rstd * (
        d_hat
        - jnp.mean(d_hat, axis=1, keepdims=True)
        - x_hat * jnp.mean(d_hat * x_hat, axis=1, keepdims=True)
    )
    d_x = d_x + dot(scatter_b, grad, NN)
    hot = d_x[0:hot_rows]
    c_scr[...] = d_x[hot_rows:slots] * live

    share = hot_rows * chunks // n_dev
    if share % SUBLANES:
        g_scr[...] = hot
    for g in range(hot_rows // SUBLANES):
        for c in range(chunks):
            first = (g * chunks + c) * SUBLANES
            at = (slice(g * SUBLANES, (g + 1) * SUBLANES), slice(c * LANES, (c + 1) * LANES))
            if share % SUBLANES == 0:
                off = first % share // 2
                out_ref[first // share, off : off + SUBLANES // 2] = hot[at].reshape(
                    SUBLANES // 2, 2, LANES
                )
            else:
                for i in range(SUBLANES):
                    to, off = divmod(first + i, share)
                    row = g * SUBLANES + i
                    out_ref[to, off // 2, off % 2 : off % 2 + 1, :] = g_scr[row : row + 1, at[1]]

    part = chunks // n_rep
    base = even(share) // 2
    for j in range(n_owner):
        for c in range(chunks):
            to = j * n_rep + c // part
            cols = slice(c * LANES, (c + 1) * LANES)
            if part == 1 and slot == 2:
                out_ref[to, base] = c_scr[j * slot : (j + 1) * slot, cols]
            else:
                for k in range(slot):
                    off = k * part + c % part
                    at = j * slot + k
                    out_ref[to, base + off // 2, off % 2 : off % 2 + 1, :] = c_scr[at : at + 1, cols]


def sum_kernel(got_ref, out_ref, cold_ref):
    n_dev, share, _ = out_ref.shape
    base = even(share) // 2
    total = got_ref[0, 0:base]
    for d in range(1, n_dev):
        total = total + got_ref[d, 0:base]
    total = total.reshape(2 * base, LANES)[0:share]
    for d in range(n_dev):
        out_ref[d] = total
    cold_ref[...] = got_ref[:, base:]


def cold_kernel(asked_ref, *refs, slot, n_rep):
    part_refs = refs[:n_rep]
    table_ref, accum_ref, new_ref, new_accum_ref, part_scr = refs[n_rep:]
    j = lax.axis_index("rows")
    p = lax.axis_index("rep")
    n_dev = asked_ref.shape[0]
    shard, width = table_ref.shape
    chunks = width // LANES
    part = chunks // n_rep
    for s in range(n_rep):
        part_scr[(p + n_rep - s) % n_rep] = part_refs[s][...]
    asked = asked_ref[:, 0, :]
    pos = lax.broadcasted_iota(jnp.int32, asked.shape, 1)
    picks = []
    for k in range(slot):
        col = jnp.sum(jnp.where(pos == j * slot + k, asked, 0), axis=1, keepdims=True)
        picks.append((lax.broadcasted_iota(jnp.int32, (n_dev, shard), 1) == col).astype(F32))
    pick = jnp.concatenate(picks, axis=0)
    grads = []
    for c in range(chunks):
        rows = []
        for k in range(slot):
            off = k * part + c % part
            rows.append(part_scr[c // part, :, off // 2, off % 2, :])
        grads.append(dot(pick, jnp.concatenate(rows, axis=0), TN, lax.Precision.HIGHEST))
    total = grads[0] * grads[0]
    for g in grads[1:]:
        total = total + g * g
    mean_sq = jnp.sum(total, axis=1, keepdims=True) * (1.0 / width)
    wide = jnp.transpose(jnp.broadcast_to(mean_sq, (shard, LANES)))
    accum_row = accum_ref[...]
    new_accum_ref[...] = accum_row + wide[0:1, :]
    accum_col = jnp.transpose(jnp.broadcast_to(accum_row, (LANES, shard)))[:, 0:1]
    step = lax.rsqrt(accum_col + mean_sq) * STEP_RATE
    for c in range(chunks):
        cols = slice(c * LANES, (c + 1) * LANES)
        new_ref[:, cols] = table_ref[:, cols] - grads[c] * step


def hot_kernel(got_ref, table_ref, accum_ref, new_ref, new_accum_ref, g_scr):
    n_dev, share, _ = got_ref.shape
    rows, width = table_ref.shape
    chunks = width // LANES
    for g in range(rows // SUBLANES):
        for c in range(chunks):
            first = (g * chunks + c) * SUBLANES
            at = (slice(g * SUBLANES, (g + 1) * SUBLANES), slice(c * LANES, (c + 1) * LANES))
            if share >= SUBLANES:
                g_scr[at] = got_ref[first // share, first % share : first % share + SUBLANES, :]
            else:
                for i in range(SUBLANES):
                    q = first + i
                    g_scr[g * SUBLANES + i : g * SUBLANES + i + 1, at[1]] = got_ref[
                        q // share, q % share : q % share + 1, :
                    ]
    grad = g_scr[...]
    mean_sq = jnp.mean(grad * grad, axis=1, keepdims=True)
    wide = jnp.transpose(jnp.broadcast_to(mean_sq, (rows, LANES)))
    accum_row = accum_ref[...]
    new_accum_ref[...] = accum_row + wide[0:1, :]
    accum_col = jnp.transpose(jnp.broadcast_to(accum_row, (LANES, rows)))[:, 0:1]
    new_ref[...] = table_ref[...] - STEP_RATE * grad * lax.rsqrt(accum_col + mean_sq)


def on_device(
    event_slots,
    fetch_rows,
    fetch_counts,
    hot_table,
    hot_accum,
    cold_table,
    cold_accum,
    ln_gain,
    ln_bias,
    w_in,
    w_out,
    out_grad,
):
    n_rows = lax.axis_size("rows")
    n_rep = lax.axis_size("rep")
    n_dev = n_rows * n_rep
    slot = fetch_rows.shape[1] // n_rows
    hot_rows, width = hot_table.shape
    shard = cold_table.shape[0]
    chunks = width // LANES
    share = hot_rows * chunks // n_dev
    cold_pairs = even(slot * (chunks // n_rep)) // 2
    asks = fetch_rows.shape[1]
    slots = hot_rows + asks

    with jax.named_scope("asks"):
        mine = pl.pallas_call(
            ask_kernel,
            out_shape=pltpu.VMEM((n_dev, 1, asks), jnp.int32),
            in_specs=[ANY],
            out_specs=VMEM,
            scratch_shapes=[pltpu.VMEM((1, asks), jnp.int32), pltpu.SemaphoreType.DMA],
            compiler_params=params(),
            cost_estimate=LONG,
            name="ask",
        )(pltpu.with_memory_space_constraint(fetch_rows, pltpu.HBM))
        asked = lax.all_to_all(mine, ALL, 0, 0, tiled=True)
    found = pl.pallas_call(
        functools.partial(gather_kernel, n_rows=n_rows, n_rep=n_rep, slot=slot),
        out_shape=jax.ShapeDtypeStruct((n_rows, slot * chunks, LANES), F32),
        in_specs=[VMEM, VMEM],
        out_specs=VMEM,
        scratch_shapes=[pltpu.VMEM((n_rows, asks), jnp.int32)],
        compiler_params=params(),
        cost_estimate=LONG,
        name="gather",
    )(asked, cold_table)
    fetched = lax.all_to_all(found, "rows", 0, 0, tiled=True)

    sent = pl.pallas_call(
        functools.partial(layer_kernel, n_dev=n_dev, n_rep=n_rep, slot=slot),
        out_shape=jax.ShapeDtypeStruct((n_dev, even(share) // 2 + cold_pairs, 2, LANES), F32),
        in_specs=[VMEM] * 9,
        out_specs=VMEM,
        scratch_shapes=[
            pltpu.VMEM((slots, width), F32),
            pltpu.VMEM((hot_rows, width), F32),
            pltpu.VMEM((asks, width), F32),
        ],
        compiler_params=params(),
        name="layer",
    )(
        event_slots,
        fetch_counts,
        hot_table,
        fetched,
        ln_gain.reshape(1, width),
        ln_bias.reshape(1, width),
        w_in,
        w_out,
        out_grad,
    )
    got = lax.all_to_all(sent, ALL, 0, 0, tiled=True)

    summed, cold_part = pl.pallas_call(
        sum_kernel,
        out_shape=(
            pltpu.VMEM((n_dev, share, LANES), F32),
            pltpu.VMEM((n_dev, cold_pairs, 2, LANES), F32),
        ),
        in_specs=[VMEM],
        out_specs=(VMEM, VMEM),
        compiler_params=params(),
        name="sum",
    )(got)
    hot_grad = lax.all_to_all(summed, ALL, 0, 0, tiled=True)
    parts = [cold_part] + [
        lax.ppermute(cold_part, "rep", [(i, (i + s) % n_rep) for i in range(n_rep)])
        for s in range(1, n_rep)
    ]

    new_cold_table, new_cold_accum = pl.pallas_call(
        functools.partial(cold_kernel, slot=slot, n_rep=n_rep),
        out_shape=(
            jax.ShapeDtypeStruct((shard, width), F32),
            jax.ShapeDtypeStruct((1, shard), F32),
        ),
        in_specs=[VMEM] * (n_rep + 3),
        out_specs=(VMEM, VMEM),
        scratch_shapes=[pltpu.VMEM((n_rep, n_dev, cold_pairs, 2, LANES), F32)],
        compiler_params=params(),
        name="cold",
    )(asked, *parts, cold_table, cold_accum.reshape(1, shard))

    new_hot_table, new_hot_accum = pl.pallas_call(
        hot_kernel,
        out_shape=(
            jax.ShapeDtypeStruct((hot_rows, width), F32),
            jax.ShapeDtypeStruct((1, hot_rows), F32),
        ),
        in_specs=[VMEM] * 3,
        out_specs=(VMEM, VMEM),
        scratch_shapes=[pltpu.VMEM((hot_rows, width), F32)],
        compiler_params=params(),
        name="hot",
    )(hot_grad, hot_table, hot_accum.reshape(1, hot_rows))
    return (
        new_hot_table,
        new_hot_accum.reshape(hot_rows),
        new_cold_table,
        new_cold_accum.reshape(shard),
    )


def solution(mesh):
    return jax.shard_map(
        on_device,
        mesh=mesh,
        in_specs=(
            P(ALL, None),
            P(ALL, None),
            P(ALL, None),
            P(),
            P(),
            P("rows", None),
            P("rows"),
            P(),
            P(),
            P(),
            P(),
            P(ALL, None),
        ),
        out_specs=(P(), P(), P("rows", None), P("rows")),
        check_vma=False,
    )
```

time: 69.5 us -> 57.4 us (0.83)
  blocking collectives: 24.2 us -> 36.6 us
  local copies, waits for them, and re-layouts: 9.49 us -> 0.06 us
  waiting for transfers between devices: 14.9 us -> 6.91 us
  starting transfers between devices: 9.91 us -> 4.5 us
  Pallas kernels: 9.78 us -> 8.2 us
    all_to_all x0 -> x1, blocking collectives: none -> 14.3 us  [on_device(): asked = lax.all_to_all(mine, ALL, 0, 0, tiled=True)]
    unnamed x26 -> x22, local copies, waits for them, and re-layouts: 8.22 us -> 0.06 us
    all_to_all x1 -> x0, starting transfers between devices: 7.33 us -> none  [on_device(): lax.all_to_all(jnp.broadcast_to(mine, (n_dev, per_row, LANES)), ALL, 0, 0...]
    all_to_all x1 -> x0, waiting for transfers between devices: 7.02 us -> none  [on_device(): lax.all_to_all(jnp.broadcast_to(mine, (n_dev, per_row, LANES)), ALL, 0, 0...]
    all_to_all x1, waiting for transfers between devices: 7.83 us -> 2.83 us  [on_device(): hot_grad = lax.all_to_all(summed, ALL, 0, 0, tiled=True)]
    ppermute x0 -> x3, waiting for transfers between devices: none -> 4.08 us  [on_device(): lax.ppermute(cold_part, 'rep', [(i, (i + s) % n_rep) for i in range(n_rep)])]
    all_to_all x1, blocking collectives: 15.1 us -> 13.1 us  [on_device(): got = lax.all_to_all(sent, ALL, 0, 0, tiled=True)]
    ppermute x0 -> x3, starting transfers between devices: none -> 1.92 us  [on_device(): lax.ppermute(cold_part, 'rep', [(i, (i + s) % n_rep) for i in range(n_rep)])]
  transfers between devices with their start and end apart: 2 -> 4, of which waited for: 2 -> 3; matrix products, arithmetic and copies ran while one was open for 0% -> 0% of each run, Pallas kernels for 4% -> 3%
where the time goes in v4:
time: 57.4 us; the launch traced here: 57.1 us
  blocking collectives  36.6 us (64%)
  Pallas kernels  8.2 us (14%)
  waiting for transfers between devices  6.91 us (12%)
  starting transfers between devices  4.5 us (8%)
  between operations  0.78 us (1%)
    all_to_all x1, blocking collectives, on_device(): asked = lax.all_to_all(mine, ALL, 0, 0, tiled=True)  14.3 us
    all_to_all x1, blocking collectives, on_device(): got = lax.all_to_all(sent, ALL, 0, 0, tiled=True)  13.1 us
    all_to_all x1, blocking collectives, on_device(): fetched = lax.all_to_all(found, 'rows', 0, 0, tiled=True)  9.19 us
    ppermute x3, waiting for transfers between devices, on_device(): lax.ppermute(cold_part, 'rep', [(i, (i + s) % n_rep) for i in range(n_rep)])  4.08 us
    pallas_call x1, Pallas kernels, on_device(): pl.pallas_call(functools.partial(layer_kernel, n_dev=n_dev, n_rep=n_rep,...  3.66 us
    all_to_all x1, waiting for transfers between devices, on_device(): hot_grad = lax.all_to_all(summed, ALL, 0, 0, tiled=True)  2.83 us
    all_to_all x1, starting transfers between devices, on_device(): hot_grad = lax.all_to_all(summed, ALL, 0, 0, tiled=True)  2.59 us
    ppermute x3, starting transfers between devices, on_device(): lax.ppermute(cold_part, 'rep', [(i, (i + s) % n_rep) for i in range(n_rep)])  1.92 us
  transfers between devices with their start and end apart: 4, of which 3 were waited for; matrix products, arithmetic and copies ran while one was open for 0% of the time, Pallas kernels for 3%

profile of v4, /device:TPU:0, one launch (start us, length us, event | category | flops | bytes accessed | tf_op | source)
XLA Modules:
  0.0 57.1 jit_solution(1465662496340029369)
XLA Ops:
  0.6 0.7 %ask.1 = s32[32,1,16]{2,1,0:T(1,128)S(1)} custom-call(s32[1,16]{1,0:T(1,128)} %rows_hbm.1), custom_call_target="tpu_custom_call" | custom-call | flops 10000000000 | bytes 16777216 | tf_op jit(solution)/shard_map/asks/ask/pallas_call | solution.py:334
  1.4 14.3 %all_to_all.20.asked_ref = s32[32,1,16]{2,1,0:T(1,128)S(1)} all-to-all(s32[32,1,16]{2,1,0:T(1,128)S(1)} %ask.1), channel_id=1, replica_groups=mesh['rows'=8,'rep'=4] {'rows','rep'}, dimensions={0} | all-to-all | bytes 4096 | tf_op jit(solution)/shard_map/asks/all_to_all | solution.py:344
  15.7 0.0 copy-start.4
  15.7 0.0 copy-start.5
  15.7 0.0 copy-start.6
  15.7 0.0 copy-start.8
  15.8 0.0 copy-start.9
  15.8 0.3 gather.1
  16.1 9.2 %all_to_all.21.fetched_ref = f32[8,8,128]{2,1,0:T(8,128)S(1)} all-to-all(f32[8,8,128]{2,1,0:T(8,128)S(1)} %gather.1), channel_id=1, replica_groups=mesh['rows'=8,'rep'=4] {'rows'}, dimensions={0} | all-to-all | bytes 65536 | tf_op jit(solution)/shard_map/all_to_all | solution.py:355
  25.3 0.0 copy-start.7
  25.3 0.0 copy-start.10
  25.4 3.7 %layer.1 = f32[32,9,2,128]{3,2,1,0:T(2,128)S(1)} custom-call(s32[1,128]{1,0:T(1,128)S(1)} %copy-done.8, s32[1,8]{1,0:T(1,128)S(1)} %copy-done.9, f32[128,512]{1,0:T(8,128)S(1)} %copy-done.1, f32[8,8,128]{2,1,0:T(8,128)S(1)} %all_to_all.21.fetched_ref, f32[1,512]{1,0:T(1,128)S(1)} %bitcast.6, f32[1,512]{1,0:T(1,128)S(1)} %bitcast.7, ...), custom_call_target="tpu_custom_call" | custom-call | tf_op jit(solution)/shard_map/layer/pallas_call | solution.py:357
  29.0 13.1 %all_to_all.22.got_ref = f32[32,9,2,128]{3,2,1,0:T(2,128)S(1)} all-to-all(f32[32,9,2,128]{3,2,1,0:T(2,128)S(1)} %layer.1), channel_id=1, replica_groups=mesh['rows'=8,'rep'=4] {'rows','rep'}, dimensions={0} | all-to-all | bytes 589824 | tf_op jit(solution)/shard_map/all_to_all | solution.py:380
  42.1 0.8 %sum.1 = (f32[32,16,128]{2,1,0:T(8,128)}, f32[32,1,2,128]{3,2,1,0:T(2,128)S(1)}) custom-call(f32[32,9,2,128]{3,2,1,0:T(2,128)S(1)} %all_to_all.22.got_ref), custom_call_target="tpu_custom_call" | custom-call | tf_op jit(solution)/shard_map/sum/pallas_call | solution.py:382
  42.9 2.6 %all-to-all-start.3 = ((f32[32,16,128]{2,1,0:T(8,128)}), f32[32,16,128]{2,1,0:T(8,128)S(1)}, u32[]{:S(2)}, u32[]{:S(2)}) async-start(f32[32,16,128]{2,1,0:T(8,128)} %get-tuple-element.10), calls=%async_computation.3 | async-start | bytes 524288 | tf_op jit(solution)/shard_map/all_to_all | solution.py:393
  45.5 1.4 %collective-permute-start.2 = (f32[32,1,2,128]{3,2,1,0:T(2,128)S(1)}, f32[32,1,2,128]{3,2,1,0:T(2,128)S(1)}, u32[]{:S(2)}, u32[]{:S(2)}) collective-permute-start(f32[32,1,2,128]{3,2,1,0:T(2,128)S(1)} %get-tuple-element.13.refs_0_), channel_id=1, source_target_pairs={{0,3},{1,0},{2,1},{3,2},{4,7},{5,4},{6,5},{7,6},{8,11},{9,8},{10,9... | collective-permute-start | bytes 98312 | tf_op jit(solution)/shard_map/ppermute | solution.py:395
  46.9 0.4 collective-permute-start.1
  47.3 0.1 collective-permute-start
  47.4 1.7 %collective-permute-done.2.refs_3_ = f32[32,1,2,128]{3,2,1,0:T(2,128)S(1)} collective-permute-done((f32[32,1,2,128]{3,2,1,0:T(2,128)S(1)}, f32[32,1,2,128]{3,2,1,0:T(2,128)S(1)}, u32[]{:S(2)}, u32[]{:S(2)}) %collective-permute-start.2) | collective-permute-done | bytes 32800 | tf_op jit(solution)/shard_map/ppermute | solution.py:395
  49.2 2.3 %collective-permute-done.1.refs_2_ = f32[32,1,2,128]{3,2,1,0:T(2,128)S(1)} collective-permute-done((f32[32,1,2,128]{3,2,1,0:T(2,128)S(1)}, f32[32,1,2,128]{3,2,1,0:T(2,128)S(1)}, u32[]{:S(2)}, u32[]{:S(2)}) %collective-permute-start.1) | collective-permute-done | bytes 32800 | tf_op jit(solution)/shard_map/ppermute | solution.py:395
  51.5 0.0 collective-permute-done.refs_1_
  51.5 1.7 %cold.1 = (f32[256,512]{1,0:T(8,128)}, f32[1,256]{1,0:T(1,128)}) custom-call(s32[32,1,16]{2,1,0:T(1,128)S(1)} %all_to_all.20.asked_ref, f32[32,1,2,128]{3,2,1,0:T(2,128)S(1)} %get-tuple-element.13.refs_0_, f32[32,1,2,128]{3,2,1,0:T(2,128)S(1)} %collective-permute-done.refs_1_, f32[32,1,2,128]{3,2,1,0:T(2,128)S(1)} %collective-permute-done.1.refs_2_, ...), custom_call_target="tpu_custom_call" | custom-call | tf_op jit(solution)/shard_map/cold/pallas_call | solution.py:399
  53.2 2.8 %all-to-all-done.3.got_ref = f32[32,16,128]{2,1,0:T(8,128)S(1)} async-done(((f32[32,16,128]{2,1,0:T(8,128)}), f32[32,16,128]{2,1,0:T(8,128)S(1)}, u32[]{:S(2)}, u32[]{:S(2)}) %all-to-all-start.3) | async-done | bytes 262176 | tf_op jit(solution)/shard_map/all_to_all | solution.py:393
  56.1 1.0 %hot.1 = (f32[128,512]{1,0:T(8,128)}, f32[1,128]{1,0:T(1,128)}) custom-call(f32[32,16,128]{2,1,0:T(8,128)S(1)} %all-to-all-done.3.got_ref, f32[128,512]{1,0:T(8,128)S(1)} %copy-done.1, f32[1,128]{1,0:T(1,128)S(1)} %bitcast.9), custom_call_target="tpu_custom_call" | custom-call | tf_op jit(solution)/shard_map/hot/pallas_call | solution.py:412
  (15 shorter events, 0.0 us)
Async XLA Ops:
  0.6 15.1 %copy-start.2 = (f32[256,512]{1,0:T(8,128)S(1)}, f32[256,512]{1,0:T(8,128)}, u32[]{:S(2)}) copy-start(f32[256,512]{1,0:T(8,128)} %refs_4_.1) | copy-start | bytes 1572868
  15.7 9.6 %copy-start = (bf16[512,2048]{1,0:T(8,128)(2,1)S(1)}, bf16[512,2048]{1,0:T(8,128)(2,1)}, u32[]{:S(2)}) copy-start(bf16[512,2048]{1,0:T(8,128)(2,1)} %w_in_ref.1) | copy-start | bytes 6291460
  15.7 9.6 %copy-start.1 = (f32[128,512]{1,0:T(8,128)S(1)}, f32[128,512]{1,0:T(8,128)}, u32[]{:S(2)}) copy-start(f32[128,512]{1,0:T(8,128)} %table_ref.3) | copy-start | bytes 786436
  15.7 9.6 %copy-start.3 = (bf16[512,512]{1,0:T(8,128)(2,1)S(1)}, bf16[512,512]{1,0:T(8,128)(2,1)}, u32[]{:S(2)}) copy-start(bf16[512,512]{1,0:T(8,128)(2,1)} %w_out_ref.1) | copy-start | bytes 1572868
  15.7 9.6 %copy-start.4 = (bf16[128,512]{1,0:T(8,128)(2,1)S(1)}, bf16[128,512]{1,0:T(8,128)(2,1)}, u32[]{:S(2)}) copy-start(bf16[128,512]{1,0:T(8,128)(2,1)} %grad_ref.1) | copy-start | bytes 393220
  15.7 9.6 %copy-start.5 = (f32[512]{0:T(512)S(1)}, f32[512]{0:T(512)}, u32[]{:S(2)}) copy-start(f32[512]{0:T(512)} %param.19) | copy-start | bytes 6148
  15.7 9.6 %copy-start.6 = (f32[512]{0:T(512)S(1)}, f32[512]{0:T(512)}, u32[]{:S(2)}) copy-start(f32[512]{0:T(512)} %param.20) | copy-start | bytes 6148
  15.7 9.6 %copy-start.8 = (s32[1,128]{1,0:T(1,128)S(1)}, s32[1,128]{1,0:T(1,128)}, u32[]{:S(2)}) copy-start(s32[1,128]{1,0:T(1,128)} %event_ref.1) | copy-start | bytes 1540
  15.8 9.6 %copy-start.9 = (s32[1,8]{1,0:T(1,128)S(1)}, s32[1,8]{1,0:T(1,128)}, u32[]{:S(2)}) copy-start(s32[1,8]{1,0:T(1,128)} %count_ref.1) | copy-start | bytes 100
  25.3 26.2 %copy-start.7 = (f32[256]{0:T(256)S(1)}, f32[256]{0:T(256)}, u32[]{:S(2)}) copy-start(f32[256]{0:T(256)} %param.18) | copy-start | bytes 3076
  25.3 30.7 %copy-start.10 = (f32[128]{0:T(128)S(1)}, f32[128]{0:T(128)}, u32[]{:S(2)}) copy-start(f32[128]{0:T(128)} %param.16) | copy-start | bytes 1540
  42.9 13.2 %all-to-all-start.3 = ((f32[32,16,128]{2,1,0:T(8,128)}), f32[32,16,128]{2,1,0:T(8,128)S(1)}, u32[]{:S(2)}, u32[]{:S(2)}) async-start(f32[32,16,128]{2,1,0:T(8,128)} %get-tuple-element.10), calls=%async_computation.3 | async-start | bytes 524288 | tf_op jit(solution)/shard_map/all_to_all | solution.py:393
  45.5 3.7 %collective-permute-start.2 = (f32[32,1,2,128]{3,2,1,0:T(2,128)S(1)}, f32[32,1,2,128]{3,2,1,0:T(2,128)S(1)}, u32[]{:S(2)}, u32[]{:S(2)}) collective-permute-start(f32[32,1,2,128]{3,2,1,0:T(2,128)S(1)} %get-tuple-element.13.refs_0_), channel_id=1, source_target_pairs={{0,3},{1,0},{2,1},{3,2},{4,7},{5,4},{6,5},{7,6},{8,11},{9,8},{10,9... | collective-permute-start | bytes 98312 | tf_op jit(solution)/shard_map/ppermute | solution.py:395
  46.9 4.6 %collective-permute-start.1 = (f32[32,1,2,128]{3,2,1,0:T(2,128)S(1)}, f32[32,1,2,128]{3,2,1,0:T(2,128)S(1)}, u32[]{:S(2)}, u32[]{:S(2)}) collective-permute-start(f32[32,1,2,128]{3,2,1,0:T(2,128)S(1)} %get-tuple-element.13.refs_0_), channel_id=1, source_target_pairs={{0,2},{1,3},{2,0},{3,1},{4,6},{5,7},{6,4},{7,5},{8,10},{9,11},{10,... | collective-permute-start | bytes 98312 | tf_op jit(solution)/shard_map/ppermute | solution.py:395
  47.3 4.2 %collective-permute-start = (f32[32,1,2,128]{3,2,1,0:T(2,128)S(1)}, f32[32,1,2,128]{3,2,1,0:T(2,128)S(1)}, u32[]{:S(2)}, u32[]{:S(2)}) collective-permute-start(f32[32,1,2,128]{3,2,1,0:T(2,128)S(1)} %get-tuple-element.13.refs_0_), channel_id=1, source_target_pairs={{0,1},{1,2},{2,3},{3,0},{4,5},{5,6},{6,7},{7,4},{8,9},{9,10},{10,1... | collective-permute-start | bytes 98312 | tf_op jit(solution)/shard_map/ppermute | solution.py:395

commit v5 on v4

--- a/solution.py
+++ b/solution.py
@@ -7,11 +7,14 @@
 from jax.experimental.pallas import tpu as pltpu
 from jax.sharding import PartitionSpec as P
 
+
 HEAD = 128
 STEP_RATE = 0.5
 LANES = 128
 SUBLANES = 8
-ALL = ("rows", "rep")
+PAIR = 2
+REP = ("far", "near")
+ALL = ("rows",) + REP
 F32 = jnp.float32
 BF16 = jnp.bfloat16
 
@@ -34,6 +37,10 @@
 NN = ((1,), (0,))
 NT = ((1,), (1,))
 TN = ((0,), (0,))
+
+
+def rep_index():
+    return lax.axis_index("far") * PAIR + lax.axis_index("near")
 
 
 def ask_kernel(rows_hbm, out_ref, rows_scr, sem):
@@ -47,33 +54,31 @@
     return n + n % 2
 
 
-def gather_kernel(asked_ref, table_ref, out_ref, rows_scr, *, n_rows, n_rep, slot):
+def gather_kernel(asked_ref, table_ref, out_ref, *, n_rep, slot):
     j = lax.axis_index("rows")
-    p = lax.axis_index("rep")
-    shard = table_ref.shape[0]
-    width = table_ref.shape[1]
-    chunks = width // LANES
-
-    for r in range(n_rows):
-        rows_scr[r : r + 1, :] = asked_ref[r * n_rep + p]
-    asked = rows_scr[...]
+    p = rep_index()
+    n_dev = asked_ref.shape[0]
+    shard, width = table_ref.shape
+    part = width // LANES // n_rep
+
+    asked = asked_ref[:, 0, :]
     pos = lax.broadcasted_iota(jnp.int32, asked.shape, 1)
     picks = []
     for k in range(slot):
         col = jnp.sum(jnp.where(pos == j * slot + k, asked, 0), axis=1, keepdims=True)
-        picks.append((lax.broadcasted_iota(jnp.int32, (n_rows, shard), 1) == col).astype(F32))
+        picks.append((lax.broadcasted_iota(jnp.int32, (n_dev, shard), 1) == col).astype(F32))
     pick = jnp.concatenate(picks, axis=0).astype(BF16)
-    table = table_ref[...]
-    high = table.astype(BF16)
-    rest = table - high.astype(F32)
-    mid = rest.astype(BF16)
-    low = (rest - mid.astype(F32)).astype(BF16)
-    rows = dot(pick, high, NN) + dot(pick, mid, NN) + dot(pick, low, NN)
-    for k in range(slot):
-        for c in range(chunks):
-            out_ref[:, k * chunks + c, :] = rows[
-                k * n_rows : (k + 1) * n_rows, c * LANES : (c + 1) * LANES
-            ]
+    for c in range(part):
+        first = pl.multiple_of((p * part + c) * LANES, LANES)
+        table = table_ref[:, pl.ds(first, LANES)]
+        high = table.astype(BF16)
+        rest = table - high.astype(F32)
+        mid = rest.astype(BF16)
+        low = (rest - mid.astype(F32)).astype(BF16)
+        rows = dot(pick, high, NN) + dot(pick, mid, NN) + dot(pick, low, NN)
+        for k in range(slot):
+            off = k * part + c
+            out_ref[:, off // 2, off % 2, :] = rows[k * n_dev : (k + 1) * n_dev, :]
 
 
 def normalise(x, eps):
@@ -98,18 +103,19 @@
     w_in_ref,
     w_out_ref,
     grad_ref,
-    out_ref,
-    x_scr,
-    g_scr,
-    c_scr,
-    *,
+    *refs,
     n_dev,
     n_rep,
     slot,
+    share,
+    paired,
 ):
+    out_ref = refs[0]
+    x_scr, c_scr, hot_scr, cold_scr = refs[-4:]
     hot_rows, width = hot_ref.shape
-    n_owner = fetched_ref.shape[0]
+    n_owner = n_dev // n_rep
     chunks = width // LANES
+    part = chunks // n_rep
     slots = x_scr.shape[0]
     fetched = slots - hot_rows
     seq = grad_ref.shape[0]
@@ -124,12 +130,16 @@
     live = (lax.broadcasted_iota(jnp.int32, (fetched, 1), 0) % slot < count_col).astype(F32)
 
     for j in range(n_owner):
-        for k in range(slot):
-            at = j * slot + k
-            for c in range(chunks):
-                c_scr[at : at + 1, c * LANES : (c + 1) * LANES] = fetched_ref[
-                    j, k * chunks + c : k * chunks + c + 1, :
-                ]
+        for c in range(chunks):
+            cols = slice(c * LANES, (c + 1) * LANES)
+            frm = j * n_rep + c // part
+            if part == 1 and slot == 2:
+                c_scr[j * slot : (j + 1) * slot, cols] = fetched_ref[frm, 0]
+            else:
+                for k in range(slot):
+                    off = k * part + c % part
+                    at = j * slot + k
+                    c_scr[at : at + 1, cols] = fetched_ref[frm, off // 2, off % 2 : off % 2 + 1, :]
     x_scr[0:hot_rows, :] = hot_ref[...]
     x_scr[hot_rows:slots, :] = c_scr[...] * live
     x_hat, rstd = normalise(x_scr[...], 1e-05)
@@ -192,51 +202,60 @@
         - x_hat * jnp.mean(d_hat * x_hat, axis=1, keepdims=True)
     )
     d_x = d_x + dot(scatter_b, grad, NN)
-    hot = d_x[0:hot_rows]
-    c_scr[...] = d_x[hot_rows:slots] * live
-
-    share = hot_rows * chunks // n_dev
-    if share % SUBLANES:
-        g_scr[...] = hot
-    for g in range(hot_rows // SUBLANES):
-        for c in range(chunks):
-            first = (g * chunks + c) * SUBLANES
-            at = (slice(g * SUBLANES, (g + 1) * SUBLANES), slice(c * LANES, (c + 1) * LANES))
-            if share % SUBLANES == 0:
-                off = first % share // 2
-                out_ref[first // share, off : off + SUBLANES // 2] = hot[at].reshape(
-                    SUBLANES // 2, 2, LANES
-                )
-            else:
-                for i in range(SUBLANES):
-                    to, off = divmod(first + i, share)
-                    row = g * SUBLANES + i
-                    out_ref[to, off // 2, off % 2 : off % 2 + 1, :] = g_scr[row : row + 1, at[1]]
-
-    part = chunks // n_rep
-    base = even(share) // 2
+    for c in range(chunks):
+        cols = slice(c * LANES, (c + 1) * LANES)
+        hot_scr[c] = d_x[0:hot_rows, cols]
+        cold_scr[c] = d_x[hot_rows:slots, cols] * live
+
+    near = lax.axis_index("near")
+    if paired:
+        tiles = share // SUBLANES
+        half = tiles // PAIR
+        base = half * SUBLANES // 2
+        for to_ref, side in ((out_ref, near), (refs[1], 1 - near)):
+            for d in range(n_dev):
+                g, c = divmod(d * tiles, chunks)
+                for i in range(half):
+                    tile = hot_scr[c + side * half + i, g * SUBLANES : (g + 1) * SUBLANES, :]
+                    to_ref[d, i * SUBLANES // 2 : (i + 1) * SUBLANES // 2] = tile.reshape(
+                        SUBLANES // 2, 2, LANES
+                    )
+    else:
+        base = even(share) // 2
+        for row in range(hot_rows):
+            for c in range(chunks):
+                unit = (row // SUBLANES * chunks + c) * SUBLANES + row % SUBLANES
+                to, off = divmod(unit, share)
+                out_ref[to, off // 2, off % 2 : off % 2 + 1, :] = hot_scr[c, row : row + 1, :]
+
     for j in range(n_owner):
         for c in range(chunks):
             to = j * n_rep + c // part
-            cols = slice(c * LANES, (c + 1) * LANES)
             if part == 1 and slot == 2:
-                out_ref[to, base] = c_scr[j * slot : (j + 1) * slot, cols]
+                out_ref[to, base] = cold_scr[c, j * slot : (j + 1) * slot, :]
             else:
                 for k in range(slot):
                     off = k * part + c % part
                     at = j * slot + k
-                    out_ref[to, base + off // 2, off % 2 : off % 2 + 1, :] = c_scr[at : at + 1, cols]
-
-
-def sum_kernel(got_ref, out_ref, cold_ref):
-    n_dev, share, _ = out_ref.shape
-    base = even(share) // 2
-    total = got_ref[0, 0:base]
-    for d in range(1, n_dev):
-        total = total + got_ref[d, 0:base]
-    total = total.reshape(2 * base, LANES)[0:share]
-    for d in range(n_dev):
-        out_ref[d] = total
+                    out_ref[to, base + off // 2, off % 2 : off % 2 + 1, :] = cold_scr[c, at : at + 1, :]
+
+
+def pair_kernel(keep_ref, got_ref, out_ref):
+    base = got_ref.shape[1]
+    out_ref[:, 0:base] = keep_ref[:, 0:base] + got_ref[...]
+    out_ref[:, base:] = keep_ref[:, base:]
+
+
+def sum_kernel(got_ref, out_ref, cold_ref, *, base, sides):
+    n_dev = got_ref.shape[0]
+    share = out_ref.shape[1]
+    for side in range(sides):
+        total = got_ref[side, 0:base]
+        for d in range(side + sides, n_dev, sides):
+            total = total + got_ref[d, 0:base]
+        total = total.reshape(2 * base, LANES)[0:share]
+        for d in range(side, n_dev, sides):
+            out_ref[d] = total
     cold_ref[...] = got_ref[:, base:]
 
 
@@ -244,7 +263,7 @@
     part_refs = refs[:n_rep]
     table_ref, accum_ref, new_ref, new_accum_ref, part_scr = refs[n_rep:]
     j = lax.axis_index("rows")
-    p = lax.axis_index("rep")
+    p = rep_index()
     n_dev = asked_ref.shape[0]
     shard, width = table_ref.shape
     chunks = width // LANES
@@ -279,22 +298,31 @@
         new_ref[:, cols] = table_ref[:, cols] - grads[c] * step
 
 
-def hot_kernel(got_ref, table_ref, accum_ref, new_ref, new_accum_ref, g_scr):
-    n_dev, share, _ = got_ref.shape
+def hot_kernel(*refs, paired):
+    n_in = 1 + paired
+    table_ref, accum_ref, new_ref, new_accum_ref, g_scr = refs[n_in : n_in + 5]
     rows, width = table_ref.shape
     chunks = width // LANES
-    for g in range(rows // SUBLANES):
-        for c in range(chunks):
-            first = (g * chunks + c) * SUBLANES
-            at = (slice(g * SUBLANES, (g + 1) * SUBLANES), slice(c * LANES, (c + 1) * LANES))
-            if share >= SUBLANES:
-                g_scr[at] = got_ref[first // share, first % share : first % share + SUBLANES, :]
-            else:
-                for i in range(SUBLANES):
-                    q = first + i
-                    g_scr[g * SUBLANES + i : g * SUBLANES + i + 1, at[1]] = got_ref[
-                        q // share, q % share : q % share + 1, :
-                    ]
+    if paired:
+        own_ref, twin_ref, got_ref = refs[0], refs[1], refs[-1]
+        near = lax.axis_index("near")
+        got_ref[near] = own_ref[...]
+        got_ref[1 - near] = twin_ref[...]
+        half = own_ref.shape[1] // SUBLANES
+        for tile in range(rows // SUBLANES * chunks):
+            g, c = divmod(tile, chunks)
+            d, i = divmod(tile, PAIR * half)
+            off = i % half * SUBLANES
+            g_scr[g * SUBLANES : (g + 1) * SUBLANES, c * LANES : (c + 1) * LANES] = got_ref[
+                i // half, d, off : off + SUBLANES, :
+            ]
+    else:
+        share = refs[0].shape[1]
+        for row in range(rows):
+            for c in range(chunks):
+                unit = (row // SUBLANES * chunks + c) * SUBLANES + row % SUBLANES
+                frm, off = divmod(unit, share)
+                g_scr[row : row + 1, c * LANES : (c + 1) * LANES] = refs[0][frm, off : off + 1, :]
     grad = g_scr[...]
     mean_sq = jnp.mean(grad * grad, axis=1, keepdims=True)
     wide = jnp.transpose(jnp.broadcast_to(mean_sq, (rows, LANES)))
@@ -319,50 +347,57 @@
     out_grad,
 ):
     n_rows = lax.axis_size("rows")
-    n_rep = lax.axis_size("rep")
+    n_rep = lax.axis_size("far") * PAIR
     n_dev = n_rows * n_rep
     slot = fetch_rows.shape[1] // n_rows
     hot_rows, width = hot_table.shape
     shard = cold_table.shape[0]
     chunks = width // LANES
     share = hot_rows * chunks // n_dev
+    tiles = share // SUBLANES
+    paired = share % (PAIR * SUBLANES) == 0 and chunks % max(tiles, 1) == 0
+    sides = PAIR if paired else 1
+    unit = share // sides
+    base = even(unit) // 2
     cold_pairs = even(slot * (chunks // n_rep)) // 2
     asks = fetch_rows.shape[1]
     slots = hot_rows + asks
 
-    with jax.named_scope("asks"):
-        mine = pl.pallas_call(
-            ask_kernel,
-            out_shape=pltpu.VMEM((n_dev, 1, asks), jnp.int32),
-            in_specs=[ANY],
-            out_specs=VMEM,
-            scratch_shapes=[pltpu.VMEM((1, asks), jnp.int32), pltpu.SemaphoreType.DMA],
-            compiler_params=params(),
-            cost_estimate=LONG,
-            name="ask",
-        )(pltpu.with_memory_space_constraint(fetch_rows, pltpu.HBM))
-        asked = lax.all_to_all(mine, ALL, 0, 0, tiled=True)
+    mine = pl.pallas_call(
+        ask_kernel,
+        out_shape=pltpu.VMEM((n_dev, 1, asks), jnp.int32),
+        in_specs=[ANY],
+        out_specs=VMEM,
+        scratch_shapes=[pltpu.VMEM((1, asks), jnp.int32), pltpu.SemaphoreType.DMA],
+        compiler_params=params(),
+        cost_estimate=LONG,
+        name="ask",
+    )(pltpu.with_memory_space_constraint(fetch_rows, pltpu.HBM))
+    asked = lax.all_to_all(mine, ALL, 0, 0, tiled=True)
     found = pl.pallas_call(
-        functools.partial(gather_kernel, n_rows=n_rows, n_rep=n_rep, slot=slot),
-        out_shape=jax.ShapeDtypeStruct((n_rows, slot * chunks, LANES), F32),
+        functools.partial(gather_kernel, n_rep=n_rep, slot=slot),
+        out_shape=jax.ShapeDtypeStruct((n_dev, cold_pairs, 2, LANES), F32),
         in_specs=[VMEM, VMEM],
         out_specs=VMEM,
-        scratch_shapes=[pltpu.VMEM((n_rows, asks), jnp.int32)],
         compiler_params=params(),
         cost_estimate=LONG,
         name="gather",
     )(asked, cold_table)
-    fetched = lax.all_to_all(found, "rows", 0, 0, tiled=True)
-
+    fetched = lax.all_to_all(found, ALL, 0, 0, tiled=True)
+
+    out = [(n_dev, base + cold_pairs, 2, LANES)] + [(n_dev, base, 2, LANES)] * paired
     sent = pl.pallas_call(
-        functools.partial(layer_kernel, n_dev=n_dev, n_rep=n_rep, slot=slot),
-        out_shape=jax.ShapeDtypeStruct((n_dev, even(share) // 2 + cold_pairs, 2, LANES), F32),
+        functools.partial(
+            layer_kernel, n_dev=n_dev, n_rep=n_rep, slot=slot, share=share, paired=paired
+        ),
+        out_shape=[jax.ShapeDtypeStruct(x, F32) for x in out],
         in_specs=[VMEM] * 9,
-        out_specs=VMEM,
+        out_specs=[VMEM] * len(out),
         scratch_shapes=[
             pltpu.VMEM((slots, width), F32),
-            pltpu.VMEM((hot_rows, width), F32),
             pltpu.VMEM((asks, width), F32),
+            pltpu.VMEM((chunks, hot_rows, LANES), F32),
+            pltpu.VMEM((chunks, asks, LANES), F32),
         ],
         compiler_params=params(),
         name="layer",
@@ -377,12 +412,23 @@
         w_out,
         out_grad,
     )
-    got = lax.all_to_all(sent, ALL, 0, 0, tiled=True)
+    swap = [(i, 1 - i) for i in range(PAIR)]
+    both = sent[0]
+    if paired:
+        both = pl.pallas_call(
+            pair_kernel,
+            out_shape=jax.ShapeDtypeStruct(out[0], F32),
+            in_specs=[VMEM] * 2,
+            out_specs=VMEM,
+            compiler_params=params(),
+            name="pair",
+        )(both, lax.ppermute(sent[1], "near", swap))
+    got = lax.all_to_all(both, ALL, 0, 0, tiled=True)
 
     summed, cold_part = pl.pallas_call(
-        sum_kernel,
+        functools.partial(sum_kernel, base=base, sides=sides),
         out_shape=(
-            pltpu.VMEM((n_dev, share, LANES), F32),
+            pltpu.VMEM((n_dev, unit, LANES), F32),
             pltpu.VMEM((n_dev, cold_pairs, 2, LANES), F32),
         ),
         in_specs=[VMEM],
@@ -390,12 +436,12 @@
         compiler_params=params(),
         name="sum",
     )(got)
-    hot_grad = lax.all_to_all(summed, ALL, 0, 0, tiled=True)
+    own = lax.all_to_all(summed, ALL, 0, 0, tiled=True)
+    grads = [own] + [lax.ppermute(own, "near", swap)] * paired
     parts = [cold_part] + [
-        lax.ppermute(cold_part, "rep", [(i, (i + s) % n_rep) for i in range(n_rep)])
+        lax.ppermute(cold_part, REP, [(i, (i + s) % n_rep) for i in range(n_rep)])
         for s in range(1, n_rep)
     ]
-
     new_cold_table, new_cold_accum = pl.pallas_call(
         functools.partial(cold_kernel, slot=slot, n_rep=n_rep),
         out_shape=(
@@ -410,17 +456,18 @@
     )(asked, *parts, cold_table, cold_accum.reshape(1, shard))
 
     new_hot_table, new_hot_accum = pl.pallas_call(
-        hot_kernel,
+        functools.partial(hot_kernel, paired=paired),
         out_shape=(
             jax.ShapeDtypeStruct((hot_rows, width), F32),
             jax.ShapeDtypeStruct((1, hot_rows), F32),
         ),
-        in_specs=[VMEM] * 3,
+        in_specs=[VMEM] * (len(grads) + 2),
         out_specs=(VMEM, VMEM),
-        scratch_shapes=[pltpu.VMEM((hot_rows, width), F32)],
+        scratch_shapes=[pltpu.VMEM((hot_rows, width), F32)]
+        + [pltpu.VMEM((PAIR, n_dev, unit, LANES), F32)] * paired,
         compiler_params=params(),
         name="hot",
-    )(hot_grad, hot_table, hot_accum.reshape(1, hot_rows))
+    )(*grads, hot_table, hot_accum.reshape(1, hot_rows))
     return (
         new_hot_table,
         new_hot_accum.reshape(hot_rows),
@@ -430,9 +477,11 @@
 
 
 def solution(mesh):
+    n_rows, n_rep = mesh.shape["rows"], mesh.shape["rep"]
+    devices = mesh.devices.reshape(n_rows, n_rep // PAIR, PAIR)
     return jax.shard_map(
         on_device,
-        mesh=mesh,
+        mesh=jax.sharding.Mesh(devices, ALL),
         in_specs=(
             P(ALL, None),
             P(ALL, None),

time: 57.4 us -> 59.5 us (1.037)
  blocking collectives: 36.6 us -> 43.9 us
  waiting for transfers between devices: 6.91 us -> 4.58 us
  starting transfers between devices: 4.5 us -> 2.32 us
    all_to_all x2 -> x3, blocking collectives: 22.3 us -> 29.6 us  [the longest x1 10.3 us: on_device(): got = lax.all_to_all(both, ALL, 0, 0, tiled=True)]
    all_to_all x1 -> x0, waiting for transfers between devices: 2.83 us -> none  [on_device(): hot_grad = lax.all_to_all(summed, ALL, 0, 0, tiled=True)]
    all_to_all x1 -> x0, starting transfers between devices: 2.59 us -> none  [on_device(): hot_grad = lax.all_to_all(summed, ALL, 0, 0, tiled=True)]
    pallas_call x3 -> x4, Pallas kernels: 2.07 us -> 1.43 us  [the longest x1 1.05 us: on_device(): pl.pallas_call(functools.partial(hot_kernel, paired=paired), out_shape=(j...]
    ppermute x3 -> x5, waiting for transfers between devices: 4.08 us -> 4.58 us  [the longest x3 3.34 us: on_device(): lax.ppermute(cold_part, REP, [(i, (i + s) % n_rep) for i in range(n_rep)])]
    ppermute x3 -> x5, starting transfers between devices: 1.92 us -> 2.32 us  [the longest x3 1.93 us: on_device(): lax.ppermute(cold_part, REP, [(i, (i + s) % n_rep) for i in range(n_rep)])]
  transfers between devices with their start and end apart: 4 -> 5, of which waited for: 3 -> 3; matrix products, arithmetic and copies ran while one was open for 0% -> 0% of each run, Pallas kernels for 3% -> 3%
where the time goes in v5:
time: 59.5 us; the launch traced here: 59.2 us
  blocking collectives  43.9 us (74%)
  Pallas kernels  7.63 us (13%)
  waiting for transfers between devices  4.58 us (8%)
  starting transfers between devices  2.32 us (4%)
  between operations  0.78 us (1%)
    all_to_all x1, blocking collectives, on_device(): asked = lax.all_to_all(mine, ALL, 0, 0, tiled=True)  14.3 us
    all_to_all x1, blocking collectives, on_device(): got = lax.all_to_all(both, ALL, 0, 0, tiled=True)  10.3 us
    all_to_all x1, blocking collectives, on_device(): own = lax.all_to_all(summed, ALL, 0, 0, tiled=True)  10.2 us
    all_to_all x1, blocking collectives, on_device(): fetched = lax.all_to_all(found, ALL, 0, 0, tiled=True)  9.08 us
    pallas_call x1, Pallas kernels, on_device(): pl.pallas_call(functools.partial(layer_kernel, n_dev=n_dev, n_rep=n_rep,...  3.72 us
    ppermute x3, waiting for transfers between devices, on_device(): lax.ppermute(cold_part, REP, [(i, (i + s) % n_rep) for i in range(n_rep)])  3.34 us
    ppermute x3, starting transfers between devices, on_device(): lax.ppermute(cold_part, REP, [(i, (i + s) % n_rep) for i in range(n_rep)])  1.93 us
    pallas_call x1, Pallas kernels, on_device(): pl.pallas_call(functools.partial(cold_kernel, slot=slot, n_rep=n_rep), ou...  1.75 us
  transfers between devices with their start and end apart: 5, of which 3 were waited for; matrix products, arithmetic and copies ran while one was open for 0% of the time, Pallas kernels for 3%

profile of v5, /device:TPU:0, one launch (start us, length us, event | category | flops | bytes accessed | tf_op | source)
XLA Modules:
  0.0 59.2 jit_solution(2113844573668833548)
XLA Ops:
  0.6 0.7 %ask.1 = s32[32,1,16]{2,1,0:T(1,128)S(1)} custom-call(s32[1,16]{1,0:T(1,128)} %rows_hbm.1), custom_call_target="tpu_custom_call" | custom-call | flops 10000000000 | bytes 16777216 | tf_op jit(solution)/shard_map/ask/pallas_call | solution.py:366
  1.4 14.3 %all_to_all.20.asked_ref = s32[32,1,16]{2,1,0:T(1,128)S(1)} all-to-all(s32[32,1,16]{2,1,0:T(1,128)S(1)} %ask.1), channel_id=1, replica_groups=mesh['rows'=8,'far'=2,'near'=2] {'rows','far','near'}, dimensions={0} | all-to-all | bytes 4096 | tf_op jit(solution)/shard_map/all_to_all | solution.py:376
  15.7 0.0 copy-start.4
  15.7 0.0 copy-start.5
  15.7 0.0 copy-start.6
  15.7 0.0 copy-start.9
  15.8 0.0 copy-start.10
  15.8 0.3 gather.1
  16.0 9.1 %all_to_all.21.fetched_ref = f32[32,1,2,128]{3,2,1,0:T(2,128)S(1)} all-to-all(f32[32,1,2,128]{3,2,1,0:T(2,128)S(1)} %gather.1), channel_id=1, replica_groups=mesh['rows'=8,'far'=2,'near'=2] {'rows','far','near'}, dimensions={0} | all-to-all | bytes 65536 | tf_op jit(solution)/shard_map/all_to_all | solution.py:386
  25.2 0.0 copy-start.7
  25.2 0.0 copy-start.8
  25.2 3.7 %layer.1 = (f32[32,5,2,128]{3,2,1,0:T(2,128)S(1)}, f32[32,4,2,128]{3,2,1,0:T(2,128)S(1)}) custom-call(s32[1,128]{1,0:T(1,128)S(1)} %copy-done.9, s32[1,8]{1,0:T(1,128)S(1)} %copy-done.10, f32[128,512]{1,0:T(8,128)S(1)} %copy-done.1, f32[32,1,2,128]{3,2,1,0:T(2,128)S(1)} %all_to_all.21.fetched_ref, f32[1,512]{1,0:T(1,128)S(1)} %bitcast.6, ...), custom_call_target="tpu_custom_call" | custom-call | tf_op jit(solution)/shard_map/layer/pallas_call | solution.py:389
  28.9 0.2 collective-permute-start
  29.1 1.2 %collective-permute-done.got_ref = f32[32,4,2,128]{3,2,1,0:T(2,128)S(1)} collective-permute-done((f32[32,4,2,128]{3,2,1,0:T(2,128)S(1)}, f32[32,4,2,128]{3,2,1,0:T(2,128)S(1)}, u32[]{:S(2)}, u32[]{:S(2)}) %collective-permute-start) | collective-permute-done | bytes 131104 | tf_op jit(solution)/shard_map/ppermute | solution.py:425
  30.3 0.1 pair.1
  30.4 10.3 %all_to_all.22.got_ref = f32[32,5,2,128]{3,2,1,0:T(2,128)S(1)} all-to-all(f32[32,5,2,128]{3,2,1,0:T(2,128)S(1)} %pair.1), channel_id=1, replica_groups=mesh['rows'=8,'far'=2,'near'=2] {'rows','far','near'}, dimensions={0} | all-to-all | bytes 327680 | tf_op jit(solution)/shard_map/all_to_all | solution.py:426
  40.8 10.2 %all_to_all.23.refs_0_ = f32[32,8,128]{2,1,0:T(8,128)S(1)} all-to-all(f32[32,8,128]{2,1,0:T(8,128)S(1)} %get-tuple-element.14), channel_id=1, replica_groups=mesh['rows'=8,'far'=2,'near'=2] {'rows','far','near'}, dimensions={0} | all-to-all | bytes 262144 | tf_op jit(solution)/shard_map/all_to_all | solution.py:439
  51.0 0.2 collective-permute-start.1
  51.2 0.2 collective-permute-start.4
  51.4 1.7 %collective-permute-start.3 = (f32[32,1,2,128]{3,2,1,0:T(2,128)S(1)}, f32[32,1,2,128]{3,2,1,0:T(2,128)S(1)}, u32[]{:S(2)}, u32[]{:S(2)}) collective-permute-start(f32[32,1,2,128]{3,2,1,0:T(2,128)S(1)} %get-tuple-element.17.refs_0_), channel_id=1, source_target_pairs={{0,2},{1,3},{2,0},{3,1},{4,6},{5,7},{6,4},{7,5},{8,10},{9,11},{10,... | collective-permute-start | bytes 98312 | tf_op jit(solution)/shard_map/ppermute | solution.py:442
  53.1 2.2 %collective-permute-done.3.refs_2_ = f32[32,1,2,128]{3,2,1,0:T(2,128)S(1)} collective-permute-done((f32[32,1,2,128]{3,2,1,0:T(2,128)S(1)}, f32[32,1,2,128]{3,2,1,0:T(2,128)S(1)}, u32[]{:S(2)}, u32[]{:S(2)}) %collective-permute-start.3) | collective-permute-done | bytes 32800 | tf_op jit(solution)/shard_map/ppermute | solution.py:442
  55.3 1.1 %collective-permute-done.2.refs_1_ = f32[32,1,2,128]{3,2,1,0:T(2,128)S(1)} collective-permute-done((f32[32,1,2,128]{3,2,1,0:T(2,128)S(1)}, f32[32,1,2,128]{3,2,1,0:T(2,128)S(1)}, u32[]{:S(2)}, u32[]{:S(2)}) %collective-permute-start.2) | collective-permute-done | bytes 32800 | tf_op jit(solution)/shard_map/ppermute | solution.py:442
  56.4 1.7 %cold.1 = (f32[256,512]{1,0:T(8,128)}, f32[1,256]{1,0:T(1,128)}) custom-call(s32[32,1,16]{2,1,0:T(1,128)S(1)} %all_to_all.20.asked_ref, f32[32,1,2,128]{3,2,1,0:T(2,128)S(1)} %get-tuple-element.17.refs_0_, f32[32,1,2,128]{3,2,1,0:T(2,128)S(1)} %collective-permute-done.2.refs_1_, f32[32,1,2,128]{3,2,1,0:T(2,128)S(1)} %collective-permute-done.3.refs_2_, ...), custom_call_target="tpu_custom_call" | custom-call | tf_op jit(solution)/shard_map/cold/pallas_call | solution.py:445
  58.2 1.0 %hot.1 = (f32[128,512]{1,0:T(8,128)}, f32[1,128]{1,0:T(1,128)}) custom-call(f32[32,8,128]{2,1,0:T(8,128)S(1)} %all_to_all.23.refs_0_, f32[32,8,128]{2,1,0:T(8,128)S(1)} %collective-permute-done.1.refs_1_, f32[128,512]{1,0:T(8,128)S(1)} %copy-done.1, f32[1,128]{1,0:T(1,128)S(1)} %bitcast.9), custom_call_target="tpu_custom_call" | custom-call | tf_op jit(solution)/shard_map/hot/pallas_call | solution.py:458
  (19 shorter events, 0.1 us)
Async XLA Ops:
  0.6 15.1 %copy-start.2 = (f32[256,512]{1,0:T(8,128)S(1)}, f32[256,512]{1,0:T(8,128)}, u32[]{:S(2)}) copy-start(f32[256,512]{1,0:T(8,128)} %refs_4_.1) | copy-start | bytes 1572868
  15.7 9.4 %copy-start = (bf16[512,2048]{1,0:T(8,128)(2,1)S(1)}, bf16[512,2048]{1,0:T(8,128)(2,1)}, u32[]{:S(2)}) copy-start(bf16[512,2048]{1,0:T(8,128)(2,1)} %w_in_ref.1) | copy-start | bytes 6291460
  15.7 9.4 %copy-start.1 = (f32[128,512]{1,0:T(8,128)S(1)}, f32[128,512]{1,0:T(8,128)}, u32[]{:S(2)}) copy-start(f32[128,512]{1,0:T(8,128)} %refs_2_.1) | copy-start | bytes 786436
  15.7 9.4 %copy-start.3 = (bf16[512,512]{1,0:T(8,128)(2,1)S(1)}, bf16[512,512]{1,0:T(8,128)(2,1)}, u32[]{:S(2)}) copy-start(bf16[512,512]{1,0:T(8,128)(2,1)} %w_out_ref.1) | copy-start | bytes 1572868
  15.7 9.4 %copy-start.4 = (bf16[128,512]{1,0:T(8,128)(2,1)S(1)}, bf16[128,512]{1,0:T(8,128)(2,1)}, u32[]{:S(2)}) copy-start(bf16[128,512]{1,0:T(8,128)(2,1)} %grad_ref.1) | copy-start | bytes 393220
  15.7 9.4 %copy-start.5 = (f32[512]{0:T(512)S(1)}, f32[512]{0:T(512)}, u32[]{:S(2)}) copy-start(f32[512]{0:T(512)} %param.19) | copy-start | bytes 6148
  15.7 9.4 %copy-start.6 = (f32[512]{0:T(512)S(1)}, f32[512]{0:T(512)}, u32[]{:S(2)}) copy-start(f32[512]{0:T(512)} %param.20) | copy-start | bytes 6148
  15.7 9.4 %copy-start.9 = (s32[1,128]{1,0:T(1,128)S(1)}, s32[1,128]{1,0:T(1,128)}, u32[]{:S(2)}) copy-start(s32[1,128]{1,0:T(1,128)} %event_ref.1) | copy-start | bytes 1540
  15.8 9.4 %copy-start.10 = (s32[1,8]{1,0:T(1,128)S(1)}, s32[1,8]{1,0:T(1,128)}, u32[]{:S(2)}) copy-start(s32[1,8]{1,0:T(1,128)} %count_ref.1) | copy-start | bytes 100
  25.2 31.3 %copy-start.7 = (f32[256]{0:T(256)S(1)}, f32[256]{0:T(256)}, u32[]{:S(2)}) copy-start(f32[256]{0:T(256)} %param.18) | copy-start | bytes 3076
  25.2 33.0 %copy-start.8 = (f32[128]{0:T(128)S(1)}, f32[128]{0:T(128)}, u32[]{:S(2)}) copy-start(f32[128]{0:T(128)} %param.16) | copy-start | bytes 1540
  28.9 1.4 %collective-permute-start = (f32[32,4,2,128]{3,2,1,0:T(2,128)S(1)}, f32[32,4,2,128]{3,2,1,0:T(2,128)S(1)}, u32[]{:S(2)}, u32[]{:S(2)}) collective-permute-start(f32[32,4,2,128]{3,2,1,0:T(2,128)S(1)} %get-tuple-element.13), channel_id=1, source_target_pairs={{0,1},{1,0},{2,3},{3,2},{4,5},{5,4},{6,7},{7,6},{8,9},{9,8},{10,11... | collective-permute-start | bytes 393224 | tf_op jit(solution)/shard_map/ppermute | solution.py:425
  51.0 7.2 %collective-permute-start.1 = (f32[32,8,128]{2,1,0:T(8,128)S(1)}, f32[32,8,128]{2,1,0:T(8,128)S(1)}, u32[]{:S(2)}, u32[]{:S(2)}) collective-permute-start(f32[32,8,128]{2,1,0:T(8,128)S(1)} %all_to_all.23.refs_0_), channel_id=1, source_target_pairs={{0,1},{1,0},{2,3},{3,2},{4,5},{5,4},{6,7},{7,6},{8,9},{9,8},{10,11... | collective-permute-start | bytes 393224 | tf_op jit(solution)/shard_map/ppermute | solution.py:440
  51.2 1.9 %collective-permute-start.4 = (f32[32,1,2,128]{3,2,1,0:T(2,128)S(1)}, f32[32,1,2,128]{3,2,1,0:T(2,128)S(1)}, u32[]{:S(2)}, u32[]{:S(2)}) collective-permute-start(f32[32,1,2,128]{3,2,1,0:T(2,128)S(1)} %get-tuple-element.17.refs_0_), channel_id=1, source_target_pairs={{0,3},{1,0},{2,1},{3,2},{4,7},{5,4},{6,5},{7,6},{8,11},{9,8},{10,9... | collective-permute-start | bytes 98312 | tf_op jit(solution)/shard_map/ppermute | solution.py:442
  51.4 3.9 %collective-permute-start.3 = (f32[32,1,2,128]{3,2,1,0:T(2,128)S(1)}, f32[32,1,2,128]{3,2,1,0:T(2,128)S(1)}, u32[]{:S(2)}, u32[]{:S(2)}) collective-permute-start(f32[32,1,2,128]{3,2,1,0:T(2,128)S(1)} %get-tuple-element.17.refs_0_), channel_id=1, source_target_pairs={{0,2},{1,3},{2,0},{3,1},{4,6},{5,7},{6,4},{7,5},{8,10},{9,11},{10,... | collective-permute-start | bytes 98312 | tf_op jit(solution)/shard_map/ppermute | solution.py:442
  53.1 3.3 %collective-permute-start.2 = (f32[32,1,2,128]{3,2,1,0:T(2,128)S(1)}, f32[32,1,2,128]{3,2,1,0:T(2,128)S(1)}, u32[]{:S(2)}, u32[]{:S(2)}) collective-permute-start(f32[32,1,2,128]{3,2,1,0:T(2,128)S(1)} %get-tuple-element.17.refs_0_), channel_id=1, source_target_pairs={{0,1},{1,2},{2,3},{3,0},{4,5},{5,6},{6,7},{7,4},{8,9},{9,10},{10,1... | collective-permute-start | bytes 98312 | tf_op jit(solution)/shard_map/ppermute | solution.py:442
